TPU v7x, 128 devices: a whole 4x4x4 slice. The times are simulated.
128 devices in a mesh: slab: 16 (over y, x), lev: 8 (over z, core).
Axes of the slice: x: 4, y: 4, z: 4, core: 2. Of those that a mesh axis runs over, the one named last changes fastest.
Arguments:
- ensemble: float32 [80, 32, 36864], P(None, 'lev', 'slab'), may hold values from -6 to 6
- obs_cell: int32 [2, 256], replicated, may hold values from 0 to 1179647, as said below
- obs_value: float32 [2, 256], replicated, may hold values from -6 to 6
- obs_var: float32 [2, 256], replicated, may hold values from 0.3 to 3
- obs_frac: float32 [2, 256], replicated, may hold values from 0 to 1
- loc_column: bfloat16 [2, 256, 36864], P(None, 'lev', 'slab'), may hold values from 0 to 1
- loc_level: float32 [2, 256, 32], P(None, None, 'lev'), may hold values from 0.2 to 1
Outputs:
- analysis: float32 [80, 32, 36864], P(None, 'lev', 'slab')
- prior_mean: float32 [2, 256], replicated
Inputs may be any that keep to these rules, and one draw needn't show every extreme that they name: `obs_cell`: in each block, every device's cells (a level band of 4 levels and a slab of 2304 columns) hold at least one observation, and one of them lies in the slab's last column.
All inputs are finite; a program needn't handle non-finite values.
Results may differ from a plain program's by a relative error of at most 0.0055.
Values may be sent and summed in bfloat16 or wider, within the bound.
A program may use at most 64 MiB of HBM per device.

v0:
```python
import jax
import jax.numpy as jnp
from jax import lax
from jax.sharding import PartitionSpec as P


def laid_out(parts, dim):
    parts = jnp.moveaxis(parts, 0, dim)
    shape = parts.shape
    return parts.reshape(*shape[:dim], shape[dim] * shape[dim + 1], *shape[dim + 2 :])


def sent_to_all(array, axis):
    copies = jnp.broadcast_to(array, (lax.axis_size(axis), *array.shape))
    return lax.all_to_all(copies, axis, split_axis=0, concat_axis=0, tiled=True)


def gather_directly(array, axis, dim):
    return laid_out(sent_to_all(array, axis), dim)


def obs_stats(prior_obs, obs_val, variance):
    members = prior_obs.shape[1]
    obs_mean = jnp.mean(prior_obs, axis=1)
    deviation = prior_obs - obs_mean[:, None]
    spread = jnp.sum(deviation * deviation, axis=1) / (members - 1.0)
    total_var = spread + variance
    shrink = 1.0 / (1.0 + jnp.sqrt(variance / total_var))
    gain_rows = ((obs_val - obs_mean)[:, None] - deviation * shrink[:, None]) / (
        total_var * (members - 1.0)
    )[:, None]
    return (obs_mean, deviation.astype(jnp.bfloat16), gain_rows.astype(jnp.bfloat16))


def cell_values(current, levels, columns):
    members, lev_rows, slab_cols = current.shape
    local_row = levels - lax.axis_index("lev") * lev_rows
    local_col = columns - lax.axis_index("slab") * slab_cols
    inside = (local_row >= 0) & (local_row < lev_rows) & (local_col >= 0) & (local_col < slab_cols)
    row_safe = jnp.clip(local_row, 0, lev_rows - 1)
    col_safe = jnp.clip(local_col, 0, slab_cols - 1)
    flattened = current.reshape(members, lev_rows * slab_cols)
    picked = jnp.take(flattened, row_safe * slab_cols + col_safe, axis=1)
    return jnp.where(inside[None, :], picked, 0.0).T


def column_table(loc_block, columns):
    rows_local, slab_cols = loc_block.shape
    local_col = columns - lax.axis_index("slab") * slab_cols
    inside = (local_col >= 0) & (local_col < slab_cols)
    col_safe = jnp.clip(local_col, 0, slab_cols - 1)
    picked = jnp.take(loc_block, col_safe, axis=1).astype(jnp.float32)
    picked = jnp.where(inside[None, :], picked, 0.0)
    holder = jnp.zeros((rows_local * lax.axis_size("lev"), columns.shape[0]), jnp.float32)
    return lax.dynamic_update_slice(
        holder, picked, (lax.axis_index("lev") * rows_local, jnp.int32(0))
    )


def level_table(lev_block, levels):
    lev_rows = lev_block.shape[1]
    local_row = levels - lax.axis_index("lev") * lev_rows
    inside = (local_row >= 0) & (local_row < lev_rows) & (lax.axis_index("slab") == 0)
    row_safe = jnp.clip(local_row, 0, lev_rows - 1)
    picked = jnp.take(lev_block, row_safe, axis=1)
    return jnp.where(inside[None, :], picked, 0.0)


def cell_update(values, dev_b, gain_b, col_table, lev_table):
    centred_cells = (values - jnp.mean(values, axis=1)[:, None]).astype(jnp.bfloat16)
    cross_cov = jnp.dot(dev_b, centred_cells.T, preferred_element_type=jnp.float32)
    mixed_rows = (lev_table * col_table * cross_cov).astype(jnp.bfloat16)
    return values + jnp.dot(gain_b.T, mixed_rows, preferred_element_type=jnp.float32).T


def regress_rows(running, loc_piece, row_start, centred, dev_b, gain_b, lev_weights):
    row_total = loc_piece.shape[0]
    row_step = min(row_total, 64)
    lev_rows = lev_weights.shape[1]
    slab_cols = loc_piece.shape[1]
    for offset in range(0, row_total, row_step):
        row_count = min(row_step, row_total - offset)
        row_piece = loc_piece[offset : offset + row_count]
        dev_rows = lax.dynamic_slice_in_dim(dev_b, row_start + offset, row_count, 0)
        gain_rows = lax.dynamic_slice_in_dim(gain_b, row_start + offset, row_count, 0)
        level_loc = lax.dynamic_slice_in_dim(lev_weights, row_start + offset, row_count, 0)
        cross_cov = jnp.dot(dev_rows, centred, preferred_element_type=jnp.float32).reshape(
            row_count, lev_rows, slab_cols
        )
        weights = level_loc[:, :, None] * row_piece[:, None, :].astype(jnp.float32)
        mixed_rows = (
            (weights * cross_cov).astype(jnp.bfloat16).reshape(row_count, lev_rows * slab_cols)
        )
        running = running + jnp.dot(gain_rows.T, mixed_rows, preferred_element_type=jnp.float32)
    return running


def on_device(ensemble, obs_cell, obs_value, obs_var, obs_frac, loc_column, loc_level):
    members, lev_rows, slab_cols = ensemble.shape
    n_blocks = obs_cell.shape[0]
    total_cols = slab_cols * lax.axis_size("slab")
    pair_index = {}
    pieces = []
    for later in range(n_blocks):
        levels = obs_cell[later] // total_cols
        columns = obs_cell[later] % total_cols
        next_cols = (columns + 1) % total_cols
        pieces.append(cell_values(ensemble, levels, columns))
        pieces.append(cell_values(ensemble, levels, next_cols))
        for earlier in range(later):
            pair_index[earlier, later] = len(pieces)
            pieces.append(column_table(loc_column[earlier], columns))
            pieces.append(column_table(loc_column[earlier], next_cols))
            pieces.append(level_table(loc_level[earlier], levels))
    summed = lax.psum(tuple(pieces), ("slab", "lev"))
    raw_first = []
    raw_second = []
    position = 0
    for later in range(n_blocks):
        raw_first.append(summed[position])
        raw_second.append(summed[position + 1])
        position = position + 2 + 3 * later
    columns_all = gather_directly(loc_column, "lev", 1)
    current = ensemble
    prior_means = []
    for block_index in range(n_blocks):
        fraction = obs_frac[block_index]
        prior_obs = (1.0 - fraction)[:, None] * raw_first[block_index] + fraction[
            :, None
        ] * raw_second[block_index]
        obs_mean, dev_b, gain_b = obs_stats(prior_obs, obs_value[block_index], obs_var[block_index])
        prior_means.append(obs_mean)
        centred = (
            (current - jnp.mean(current, axis=0))
            .astype(jnp.bfloat16)
            .reshape(members, lev_rows * slab_cols)
        )
        lev_weights = loc_level[block_index]
        zero_incr = jnp.zeros((members, lev_rows * slab_cols), jnp.float32)
        increment = regress_rows(
            zero_incr, columns_all[block_index], 0, centred, dev_b, gain_b, lev_weights
        )
        for later in range(block_index + 1, n_blocks):
            start_at = pair_index[block_index, later]
            col_first = summed[start_at]
            col_second = summed[start_at + 1]
            lev_table = summed[start_at + 2]
            raw_first[later] = cell_update(raw_first[later], dev_b, gain_b, col_first, lev_table)
            raw_second[later] = cell_update(raw_second[later], dev_b, gain_b, col_second, lev_table)
        current = current + increment.reshape(members, lev_rows, slab_cols)
    return (current, jnp.stack(prior_means))


def solution(mesh):
    in_specs = (
        P(None, "lev", "slab"),
        P(),
        P(),
        P(),
        P(),
        P(None, "lev", "slab"),
        P(None, None, "lev"),
    )
    out_specs = (P(None, "lev", "slab"), P())
    return jax.shard_map(
        on_device, mesh=mesh, in_specs=in_specs, out_specs=out_specs, check_vma=False
    )
```

profile of v0, /device:TPU:1, one launch (start us, length us, event | category | flops | bytes accessed | tf_op | source)
XLA Modules:
  0.0 267.5 jit_solution(16684422704884585923)
XLA Ops:
  7.2 2.6 broadcast_in_dim.147
  9.8 7.1 %all-to-all-start = ((bf16[8,2,32,2304]{3,2,1,0:T(8,128)(2,1)}), bf16[8,2,32,2304]{3,2,1,0:T(8,128)(2,1)}, u32[]{:S(2)}, u32[]{:S(2)}) async-start(bf16[8,2,32,2304]{3,2,1,0:T(8,128)(2,1)} %broadcast_in_dim.147), calls=%async_computation | async-start | bytes 4718592 | tf_op jit(solution)/shard_map/all_to_all | solution.py:15
  16.9 0.7 slice.107
  17.6 3.5 %copy.35 = f32[80,4,2304]{0,2,1:T(8,128)} copy(f32[80,4,2304]{2,1,0:T(4,128)S(1)} %copy-done) | data formatting | bytes 5898240 | tf_op args[0]
  21.1 0.6 fusion.72
  21.7 1.1 and_reduce_fusion.6
  22.8 0.6 compare_and_fusion.3
  23.4 3.7 %gather_fusion.2 = f32[256,80]{1,0:T(8,128)} fusion(f32[80,9216]{0,1:T(8,128)} %bitcast.212, s32[1024]{0:T(1024)S(1)} %pad_clamp_fusion.5), kind=kCustom, calls=%fused_computation.2.clone | custom fusion | bytes 164864 | tf_op jit(solution)/shard_map/jit(_take)/gather | solution.py:43
  27.1 3.7 %gather_fusion.1 = f32[256,80]{1,0:T(8,128)} fusion(f32[80,9216]{0,1:T(8,128)} %bitcast.213, s32[1024]{0:T(1024)S(1)} %pad_clamp_fusion.6), kind=kCustom, calls=%fused_computation.clone | custom fusion | bytes 164864 | tf_op jit(solution)/shard_map/jit(_take)/gather | solution.py:43
  30.8 0.6 compare_select_fusion.1
  31.4 0.6 compare_and_fusion.5
  32.5 3.7 %gather_fusion.3 = f32[256,80]{1,0:T(8,128)} fusion(f32[80,9216]{0,1:T(8,128)} %bitcast.214, s32[1024]{0:T(1024)S(1)} %pad_clamp_fusion.4), kind=kCustom, calls=%fused_computation.3.clone | custom fusion | bytes 164864 | tf_op jit(solution)/shard_map/jit(_take)/gather | solution.py:43
  36.2 1.0 gather_fusion
  37.1 0.9 copy.44
  38.0 1.2 copy.61
  39.3 1.5 gather_fusion.4
  40.7 0.9 copy.47
  41.6 1.3 pad_clamp_fusion.1
  42.9 3.8 %gather_fusion.5 = f32[256,80]{1,0:T(8,128)} fusion(f32[80,9216]{0,1:T(8,128)} %bitcast.215, s32[1024]{0:T(1024)} %pad_clamp_fusion.1), kind=kCustom, calls=%fused_computation.4.clone | custom fusion | bytes 164864 | tf_op jit(solution)/shard_map/jit(_take)/gather | solution.py:43
  46.7 1.2 pad_clamp_fusion
  48.0 1.6 gather_fusion.6
  49.6 0.9 copy.49
  50.5 1.7 fusion.45
  52.2 1.7 fusion.46
  53.9 0.7 and_reduce_fusion
  54.7 1.7 fusion.44
  56.4 1.7 select_bitcast_fusion
  58.1 1.5 fusion.43
  59.7 0.6 copy-done.12
  60.4 0.7 slice_bitcast_fusion.17
  61.7 1.7 subtract_convert_fusion.1
  63.4 150.0 %all-reduce.3.cloned.1.call-done = (f32[256,80]{1,0:T(8,128)}, f32[256,80]{1,0:T(8,128)}, f32[256,80]{1,0:T(8,128)}, f32[256,256]{1,0:T(8,128)}, f32[256,256]{1,...) async-done(((f32[256,80]{1,0:T(8,128)}, f32[256,80]{1,0:T(8,128)}, f32[256,80]{1,0:T(8,128)}, f32[256,256]{1,0:T(8,128)}, f32[256,256]{1,0:T(8,128)}, ...) | async-done | bytes 1114128 | tf_op jit(solution)/shard_map/psum | solution.py:115
  213.3 1.0 reduce_sum.75
  214.4 1.2 fusion.80
  215.8 1.0 reduce_sum.76
  217.1 2.3 fusion.32
  219.4 1.7 fusion.87
  221.1 0.6 pad_maximum_fusion
  221.9 0.9 divide_convert_fusion
  222.8 2.6 fusion.83
  225.5 1.2 copy-done.1
  226.8 0.6 fusion.15
  227.4 0.7 copy-done.7
  228.2 0.6 fusion.59
  230.2 0.6 fusion.13
  230.8 0.6 copy-done.20
  231.4 0.6 fusion.12
  232.1 0.6 convolution_add_fusion.5
  232.6 0.6 convolution_add_fusion.4
  233.2 2.2 convolution_add_fusion.3
  235.4 4.5 %reshape.387 = f32[80,4,2304]{2,1,0:T(4,128)} reshape(f32[80,9216]{1,0:T(8,128)} %convolution_add_fusion.3) | data formatting | bytes 5898240 | tf_op jit(solution)/shard_map/reshape | solution.py:150
  239.9 2.8 %fusion.79 = (f32[4,2304]{1,0:T(4,128)S(1)}, f32[80,4,2304]{2,1,0:T(4,128)S(1)}) fusion(f32[80,4,2304]{2,1,0:T(4,128)S(1)} %copy-done, f32[80,4,2304]{2,1,0:T(4,128)} %reshape.387), kind=kLoop, calls=%fused_computation.210 | loop fusion | flops 1465344 | bytes 8884224 | tf_op jit(solution)/shard_map/reduce_sum | solution.py:134
  243.4 0.9 copy-done.2
  244.3 0.6 fusion.11
  245.0 0.6 fusion.10
  245.8 0.6 fusion.9
  246.4 0.6 fusion.8
  247.1 0.7 copy-done.15
  247.8 0.6 fusion.54
  248.4 0.6 convolution_add_fusion.2
  249.0 0.6 convolution_add_fusion.1
  249.6 2.2 convolution_add_fusion
  251.8 4.7 %reshape.393 = f32[80,4,2304]{2,1,0:T(4,128)} reshape(f32[80,9216]{1,0:T(8,128)} %convolution_add_fusion) | data formatting | bytes 5898240 | tf_op jit(solution)/shard_map/reshape | solution.py:150
  256.4 4.2 %add.227 = f32[80,4,2304]{2,1,0:T(4,128)} add(f32[80,4,2304]{2,1,0:T(4,128)S(1)} %copy-done.3, f32[80,4,2304]{2,1,0:T(4,128)} %reshape.393) | non-fusion elementwise | flops 737280 | bytes 8847360 | tf_op jit(solution)/shard_map/add | solution.py:150
  (99 shorter events, 4.9 us)
Async XLA Ops:
  9.8 7.1 %copy-start.19 = (s32[2,256]{1,0:T(2,128)S(1)}, s32[2,256]{1,0:T(2,128)}, u32[]{:S(2)}) copy-start(s32[2,256]{1,0:T(2,128)} %param.12) | copy-start | bytes 6148
  9.8 7.1 %copy-start.13 = (bf16[2,32,2304]{2,1,0:T(8,128)(2,1)S(1)}, bf16[2,32,2304]{2,1,0:T(8,128)(2,1)}, u32[]{:S(2)}) copy-start(bf16[2,32,2304]{2,1,0:T(8,128)(2,1)} %param.16) | copy-start | bytes 884740
  9.8 7.8 %copy-start = (f32[80,4,2304]{2,1,0:T(4,128)S(1)}, f32[80,4,2304]{2,1,0:T(4,128)}, u32[]{:S(2)}) copy-start(f32[80,4,2304]{2,1,0:T(4,128)} %param.11) | copy-start | bytes 8847364
  9.8 213.0 %all-to-all-start = ((bf16[8,2,32,2304]{3,2,1,0:T(8,128)(2,1)}), bf16[8,2,32,2304]{3,2,1,0:T(8,128)(2,1)}, u32[]{:S(2)}, u32[]{:S(2)}) async-start(bf16[8,2,32,2304]{3,2,1,0:T(8,128)(2,1)} %broadcast_in_dim.147), calls=%async_computation | async-start | bytes 4718592 | tf_op jit(solution)/shard_map/all_to_all | solution.py:15
  16.8 196.5 %all-reduce.3.cloned.1.call-start = ((), (), s32[]{:S(2)}) async-start(), calls=%async_computation.1 | async-start | bytes 2621440 | tf_op jit(solution)/shard_map/psum | solution.py:115
  21.1 15.1 %copy-start.17 = (f32[2,256,4]{1,2,0:T(4,128)S(1)}, f32[2,256,4]{1,2,0:T(4,128)}, u32[]{:S(2)}) copy-start(f32[2,256,4]{1,2,0:T(4,128)} %param.17) | copy-start | bytes 24580
  49.6 8.5 %copy-start.14 = (f32[256,80]{1,0:T(8,128)S(1)}, f32[256,80]{1,0:T(8,128)}, u32[]{:S(2)}) copy-start(f32[256,80]{1,0:T(8,128)} %gather_fusion.5) | copy-start | bytes 245764
  49.6 10.0 %copy-start.25 = (pred[256]{0:T(512)(128)(4,1)S(1)}, pred[256]{0:T(512)(128)(4,1)}, u32[]{:S(2)}) copy-start(pred[256]{0:T(512)(128)(4,1)} %get-tuple-element.29) | copy-start | bytes 772
  49.6 10.1 %copy-start.24 = (pred[256]{0:T(512)(128)(4,1)S(1)}, pred[256]{0:T(512)(128)(4,1)}, u32[]{:S(2)}) copy-start(pred[256]{0:T(512)(128)(4,1)} %get-tuple-element.24) | copy-start | bytes 772
  54.6 5.8 %copy-start.18 = (f32[2,256,4]{1,2,0:T(4,128)S(1)}, f32[2,256,4]{1,2,0:T(4,128)}, u32[]{:S(2)}) copy-start(f32[2,256,4]{1,2,0:T(4,128)} %param.17) | copy-start | bytes 24580
  54.7 6.4 %copy-start.26 = (f32[2,256]{1,0:T(2,128)S(1)}, f32[2,256]{1,0:T(2,128)}, u32[]{:S(2)}) copy-start(f32[2,256]{1,0:T(2,128)} %param.15) | copy-start | bytes 6148
  54.7 6.5 %copy-start.27 = (f32[2,256]{1,0:T(2,128)S(1)}, f32[2,256]{1,0:T(2,128)}, u32[]{:S(2)}) copy-start(f32[2,256]{1,0:T(2,128)} %param.14) | copy-start | bytes 6148
  54.7 6.5 %copy-start.28 = (f32[2,256]{1,0:T(2,128)S(1)}, f32[2,256]{1,0:T(2,128)}, u32[]{:S(2)}) copy-start(f32[2,256]{1,0:T(2,128)} %param.13) | copy-start | bytes 6148
  59.6 0.7 copy-start.12
  59.7 0.7 copy-start.11
  213.3 6.1 %copy-start.10 = (f32[256,256]{1,0:T(8,128)S(1)}, f32[256,256]{1,0:T(8,128)}, u32[]{:S(2)}) copy-start(f32[256,256]{1,0:T(8,128)} %get-tuple-element.16) | copy-start | bytes 786436
  217.0 5.7 %copy-start.6 = (bf16[256,80]{1,0:T(8,128)(2,1)}, bf16[256,80]{1,0:T(8,128)(2,1)S(1)}, u32[]{:S(2)}) copy-start(bf16[256,80]{1,0:T(8,128)(2,1)S(1)} %get-tuple-element.53) | copy-start | bytes 122884
  217.1 5.7 %copy-start.8 = (bf16[256,80]{1,0:T(8,128)(2,1)}, bf16[256,80]{1,0:T(8,128)(2,1)S(1)}, u32[]{:S(2)}) copy-start(bf16[256,80]{1,0:T(8,128)(2,1)S(1)} %get-tuple-element.54) | copy-start | bytes 122884
  225.4 1.4 copy-start.1
  225.4 1.4 copy-start.9
  225.4 1.4 copy-start.23
  227.3 0.8 copy-start.7
  228.2 0.7 copy-start.22
  229.5 0.7 copy-start.21
  230.7 0.7 copy-start.20
  239.9 2.9 %copy-start.4 = (bf16[1,2,32,2304]{3,2,0,1:T(8,128)(2,1)S(1)}, bf16[1,2,32,2304]{3,2,0,1:T(8,128)(2,1)}, u32[]{:S(2)}) copy-start(bf16[1,2,32,2304]{3,2,0,1:T(8,128)(2,1)} %get-tuple-element.45) | copy-start | bytes 884740
  239.9 2.9 %copy-start.5 = (bf16[1,2,32,2304]{3,2,0,1:T(8,128)(2,1)S(1)}, bf16[1,2,32,2304]{3,2,0,1:T(8,128)(2,1)}, u32[]{:S(2)}) copy-start(bf16[1,2,32,2304]{3,2,0,1:T(8,128)(2,1)} %get-tuple-element.46) | copy-start | bytes 884740
  242.7 1.6 copy-start.2
  242.9 1.4 copy-start.16
  247.0 0.8 copy-start.15
  251.7 4.7 %copy-start.3 = (f32[80,4,2304]{2,1,0:T(4,128)S(1)}, f32[80,4,2304]{2,1,0:T(4,128)}, u32[]{:S(2)}) copy-start(f32[80,4,2304]{2,1,0:T(4,128)} %copy-done.2) | copy-start | bytes 8847364
Sparse Core Ops, SparseCore 0:
  60.5 152.7 all-reduce.2
where the time goes:
time: 269 us; the launch traced here: 267 us
  waiting for transfers between devices  150 us (56%)
  local copies, waits for them, and re-layouts  48.4 us (18%)
  other arithmetic  31.1 us (12%)
  matrix products  16.3 us (6%)
  between operations  14.6 us (5%)
  starting transfers between devices  7.07 us (3%)
    psum x1, waiting for transfers between devices, on_device(): summed = lax.psum(tuple(pieces), ('slab', 'lev'))  150 us
    gather x4, local copies, waits for them, and re-layouts, cell_values(): picked = jnp.take(flattened, row_safe * slab_cols + col_safe, axis=1)  14.8 us
    unnamed x60, local copies, waits for them, and re-layouts  10.4 us
    reshape x2, local copies, waits for them, and re-layouts, on_device(): current = current + increment.reshape(members, lev_rows, slab_cols)  9.15 us
    dot_general x8, matrix products, regress_rows(): jnp.dot(gain_rows.T, mixed_rows, preferred_element_type=jnp.float32)  7.74 us
    all_to_all x1, starting transfers between devices, sent_to_all(): return lax.all_to_all(copies, axis, split_axis=0, concat_axis=0, tiled=True)  7.07 us
    transpose x4, other arithmetic, cell_values(): return jnp.where(inside[None, :], picked, 0.0).T  6.56 us
  transfers between devices with their start and end apart: 2, of which 1 were waited for; matrix products, arithmetic and copies ran while one was open for 21% of the time, Pallas kernels for 0%

commit v1 on v0

v1 whole, which is shorter than its diff:
```python
import functools

import jax
import jax.numpy as jnp
from jax import lax
from jax.experimental import pallas as pl
from jax.experimental.pallas import tpu as pltpu
from jax.sharding import PartitionSpec as P

MESH = pl.DeviceIdType.MESH
SLOTS = 64
F32 = jnp.float32
BF16 = jnp.bfloat16


def nt_dot(a, b):
    return lax.dot_general(a, b, (((1,), (1,)), ((), ())), preferred_element_type=F32)


def count_at_least(x, step, number):
    total = jnp.zeros_like(x)
    for k in range(1, number):
        total = total + jnp.where(x >= float(k * step), 1.0, 0.0)
    return total


def split3(x):
    high = x.astype(BF16)
    rest = x - high.astype(F32)
    mid = rest.astype(BF16)
    low = (rest - mid.astype(F32)).astype(BF16)
    return high, mid, low


def exchange_kernel(
    chunks, n_slab, n_lev,
    cell_ref, value_ref, var_ref, frac_ref, level_ref, ens_hbm, loc_hbm,
    loc_out, dev_out, gain_out, mean_out,
    ens, loc, abuf, bbuf, acc,
    ens_sem, own_sem, out_sem, a_send, a_recv, b_send, b_recv, l_send, l_recv,
):
    slab = lax.axis_index("slab")
    lev = lax.axis_index("lev")
    lev_rows, members, cols = ens.shape
    n_obs = cell_ref.shape[1]
    total_cols = cols * n_slab
    half = members // 2

    barrier = pltpu.get_barrier_semaphore()
    slab_peer = [lax.rem(slab + k, n_slab) for k in range(n_slab)]
    lev_peer = [lax.rem(lev + k, n_lev) for k in range(n_lev)]
    for k in range(1, n_lev):
        pl.semaphore_signal(barrier, inc=1, device_id=(slab, lev_peer[k]), device_id_type=MESH)
    for k in range(1, n_slab):
        pl.semaphore_signal(barrier, inc=1, device_id=(slab_peer[k], lev), device_id_type=MESH)
    own_copies = [
        pltpu.make_async_copy(loc_hbm.at[b], loc.at[b, lev], own_sem.at[b]) for b in range(2)
    ]
    for copy in own_copies:
        copy.start()
    ens_copies = [
        pltpu.make_async_copy(ens_hbm.at[:, l, :], ens.at[l], ens_sem.at[l])
        for l in range(lev_rows)
    ]
    for copy in ens_copies:
        copy.start()

    slab_f = slab.astype(F32)
    lev_f = lev.astype(F32)
    rows = []
    for b in range(2):
        cell = cell_ref[pl.ds(b, 1), :].astype(F32)
        level = count_at_least(cell, total_cols, n_lev * lev_rows)
        column = cell - level * float(total_cols)
        later = column + 1.0
        later = jnp.where(later >= float(total_cols), 0.0, later)
        band = count_at_least(level, lev_rows, n_lev)
        inner = level - band * float(lev_rows)
        places = []
        for where_at in (column, later):
            in_slab = count_at_least(where_at, cols, n_slab)
            place = where_at - in_slab * float(cols) + 1.0
            places.append(jnp.where(in_slab == slab_f, place, 0.0))
        rows.append(
            [band, places[0], places[1], inner,
             value_ref[pl.ds(b, 1), :], var_ref[pl.ds(b, 1), :], frac_ref[pl.ds(b, 1), :]]
        )
    flat = rows[0] + rows[1]
    table = jnp.concatenate(flat + [jnp.zeros((128 - len(flat), n_obs), F32)], axis=0).T

    def column_of(b, i):
        return table[:, 7 * b + i : 7 * b + i + 1]

    lane = lax.broadcasted_iota(jnp.int32, (n_obs, 128), 1)
    lane_slot = jnp.where(lane < SLOTS, lane, lane - SLOTS).astype(F32)
    first_half = lane < SLOTS
    ranks = []
    slot_info = []
    for b in range(2):
        other = lax.broadcasted_iota(jnp.int32, (n_obs, n_obs), 1)
        mine = lax.broadcasted_iota(jnp.int32, (n_obs, n_obs), 0)
        earlier = (column_of(b, 0) == rows[b][0]) & (other < mine)
        rank = jnp.sum(jnp.where(earlier, 1.0, 0.0), axis=1, keepdims=True)
        ranks.append(rank)
        per_chunk = []
        for q in range(chunks):
            chosen = (column_of(b, 0) == lev_f) & (rank == lane_slot + float(SLOTS * q))

            def picked(x):
                return jnp.sum(jnp.where(chosen, x, 0.0), axis=0, keepdims=True)

            filled = picked(jnp.ones((n_obs, 128), F32))
            place = picked(jnp.where(first_half, column_of(b, 1), column_of(b, 2))) - 1.0
            inner = picked(jnp.broadcast_to(column_of(b, 3), (n_obs, 128)))
            value = picked(jnp.broadcast_to(column_of(b, 4), (n_obs, 128)))
            var = picked(jnp.broadcast_to(column_of(b, 5), (n_obs, 128))) + (1.0 - filled)
            frac = column_of(b, 6)
            weight = picked(jnp.where(first_half, 1.0 - frac, frac))
            per_chunk.append((place, inner, value, var, weight))
        slot_info.append(per_chunk)

    def loc_copy(b, which, holder, start, count, target):
        piece = loc.at[b, holder, pl.ds(start, count)]
        return pltpu.make_async_remote_copy(
            src_ref=piece, dst_ref=piece,
            send_sem=l_send.at[b, which], recv_sem=l_recv.at[b, which],
            device_id=(slab, target), device_id_type=MESH,
        )

    up = lax.rem(lev + 2, n_lev)
    down = lax.rem(lev + n_lev - 2, n_lev)
    far = lax.rem(lev + 4, n_lev)
    mate = lev + 1 - 2 * lax.rem(lev, 2)
    held = loc.shape[2]
    part = held // 2
    ring = []
    for b in range(2):
        ring.append([
            loc_copy(b, 0, lev, 0, part, up),
            loc_copy(b, 1, lev, part, part, down),
            loc_copy(b, 2, lev, part, part, up),
            loc_copy(b, 3, lev, 0, part, down),
            loc_copy(b, 4, down, 0, part, up),
            loc_copy(b, 5, up, part, part, down),
            loc_copy(b, 6, lev, 0, held, mate),
            loc_copy(b, 7, down, 0, held, mate),
            loc_copy(b, 8, up, 0, held, mate),
            loc_copy(b, 9, far, 0, held, mate),
        ])

    def ring_begin(b):
        for i in (0, 1, 2, 3, 6):
            ring[b][i].start()

    def ring_forward(b):
        ring[b][0].wait_recv()
        ring[b][4].start()
        ring[b][1].wait_recv()
        ring[b][5].start()
        ring[b][2].wait_recv()
        ring[b][7].start()
        ring[b][3].wait_recv()
        ring[b][8].start()

    def ring_finish(b):
        ring[b][4].wait_recv()
        ring[b][5].wait_recv()
        ring[b][9].start()
        for i in (6, 7, 8, 9):
            ring[b][i].wait_recv()

    def a_copy(r, k):
        return pltpu.make_async_remote_copy(
            src_ref=abuf.at[r, 0], dst_ref=abuf.at[r, k],
            send_sem=a_send.at[r, k], recv_sem=a_recv.at[r, k],
            device_id=(slab_peer[k], lev), device_id_type=MESH,
        )

    def b_copy(r, k):
        return pltpu.make_async_remote_copy(
            src_ref=bbuf.at[r, 0], dst_ref=bbuf.at[r, k],
            send_sem=b_send.at[r, k], recv_sem=b_recv.at[r, k],
            device_id=(slab, lev_peer[k]), device_id_type=MESH,
        )

    lane1 = lax.broadcasted_iota(jnp.int32, (1, 128), 1)
    low1 = lane1 < SLOTS

    def send_priors(r, cells):
        for q in range(chunks):
            weighted = cells[q] * slot_info[r][q][4]
            both = weighted + pltpu.roll(weighted, SLOTS, 1)
            abuf[r, 0, q] = jnp.where(low1, both[:half], both[half:])
        for k in range(1, n_slab):
            a_copy(r, k).start()

    def band_statistics(r):
        for k in range(1, n_slab):
            a_copy(r, k).wait_recv()
        for q in range(chunks):
            packed = abuf[r, 0, q]
            for k in range(1, n_slab):
                packed = packed + abuf[r, k, q]
            turned = pltpu.roll(packed, SLOTS, 1)
            prior = jnp.concatenate(
                [jnp.where(low1, packed, turned), jnp.where(low1, turned, packed)], axis=0
            )
            _, _, value, variance, _ = slot_info[r][q]
            mean = jnp.sum(prior, axis=0, keepdims=True) / float(members)
            deviation = prior - mean
            spread = jnp.sum(deviation * deviation, axis=0, keepdims=True) / (members - 1.0)
            total = spread + variance
            shrink = 1.0 / (1.0 + jnp.sqrt(variance / total))
            gain = ((value - mean) - deviation * shrink) / (total * (members - 1.0))
            bbuf[r, 0, q, pl.ds(0, members), :] = jnp.where(low1, deviation, gain).astype(BF16)
            high, mid, low = (x.astype(F32) for x in split3(mean))
            row = lax.broadcasted_iota(jnp.int32, (16, 128), 0)
            parts = jnp.where(row == 0, high, jnp.where(row == 1, mid, jnp.where(row == 2, low, 0.0)))
            bbuf[r, 0, q, pl.ds(members, 16), :] = parts.astype(BF16)
        for k in range(1, n_lev):
            b_copy(r, k).start()

    def obs_order(r):
        away = lev_f - column_of(r, 0)
        away = jnp.where(away < 0.0, away + float(n_lev), away)
        to_dev = []
        to_gain = []
        for k in range(n_lev):
            for q in range(chunks):
                chosen = (away == float(k)) & (ranks[r] == lane_slot + float(SLOTS * q))
                to_dev.append(jnp.where(chosen & first_half, 1.0, 0.0).astype(BF16))
                to_gain.append(jnp.where(chosen & ~first_half, 1.0, 0.0).astype(BF16))
        return jnp.concatenate(to_dev, axis=1), jnp.concatenate(to_gain, axis=1)

    def all_statistics(r, to_dev, to_gain):
        for k in range(1, n_lev):
            b_copy(r, k).wait_recv()
        packed = jnp.concatenate(
            [bbuf[r, k, q] for k in range(n_lev) for q in range(chunks)], axis=1
        )
        dev = nt_dot(to_dev, packed)[:, :members].astype(BF16)
        gain = nt_dot(packed[:members], to_gain).astype(BF16)
        means = nt_dot(packed[members:], to_dev)
        dev_out[r] = dev
        gain_out[r] = gain
        mean_out[pl.ds(r, 1), :] = means[0:1] + means[1:2] + means[2:3]
        return dev, gain

    wide = 256 * chunks
    places = jnp.concatenate(
        [slot_info[b][q][0] for b in range(2) for q in range(chunks)], axis=1
    )
    inners = jnp.concatenate(
        [slot_info[b][q][1] for b in range(2) for q in range(chunks)], axis=1
    )
    at_level = [jnp.where(inners == float(l), places, -1.0) for l in range(lev_rows)]
    acc[...] = jnp.zeros_like(acc)

    pl.semaphore_wait(barrier, n_lev + n_slab - 2)
    own_copies[0].wait()
    ring_begin(0)
    for copy in ens_copies:
        copy.wait()

    step_cols = 256

    def gather_step(c, carry):
        base = c * step_cols
        here = pl.ds(pl.multiple_of(base, step_cols), step_cols)
        index = (lax.broadcasted_iota(jnp.int32, (step_cols, wide), 0) + base).astype(F32)
        hot = jnp.concatenate(
            [jnp.where(index == at_level[l], 1.0, 0.0).astype(BF16) for l in range(lev_rows)],
            axis=0,
        )
        pieces = [split3(ens[l, :, here]) for l in range(lev_rows)]
        left = jnp.concatenate(
            [jnp.concatenate([pieces[l][i] for l in range(lev_rows)], axis=1) for i in range(3)],
            axis=0,
        )
        acc[...] += jnp.dot(left, hot, preferred_element_type=F32)
        return carry

    lax.fori_loop(0, cols // step_cols, gather_step, 0)
    picked_cells = acc[:members] + acc[members : 2 * members] + acc[2 * members :]
    cells = [
        [picked_cells[:, 128 * (b * chunks + q) : 128 * (b * chunks + q + 1)] for q in range(chunks)]
        for b in range(2)
    ]

    send_priors(0, cells[0])
    ring_forward(0)
    own_copies[1].wait()
    to_dev, to_gain = obs_order(0)
    band_statistics(0)
    ring_finish(0)

    later_places = jnp.concatenate([slot_info[1][q][0] for q in range(chunks)], axis=1)
    later_inners = jnp.concatenate([slot_info[1][q][1] for q in range(chunks)], axis=1)
    narrow = 128 * chunks
    index = lax.broadcasted_iota(jnp.int32, (cols, narrow), 0).astype(F32)
    hot = jnp.where(index == later_places, 1.0, 0.0).astype(BF16)
    weights = jnp.dot(loc[0].reshape(n_obs, cols), hot, preferred_element_type=F32)
    level_weight = jnp.zeros((n_obs, narrow), F32)
    for l in range(lev_rows):
        level_weight = jnp.where(later_inners == float(l), level_ref[0, :, l : l + 1], level_weight)
    weights = level_weight * weights

    dev, gain = all_statistics(0, to_dev, to_gain)
    ring_begin(1)
    now = jnp.concatenate(cells[1], axis=1)
    centred = (now - jnp.sum(now, axis=0, keepdims=True) / float(members)).astype(BF16)
    cross = jnp.dot(dev, centred, preferred_element_type=F32)
    mixed = (weights * cross).astype(BF16)
    now = now + jnp.dot(gain, mixed, preferred_element_type=F32)
    send_priors(1, [now[:, 128 * q : 128 * (q + 1)] for q in range(chunks)])

    out_copies = [pltpu.make_async_copy(loc.at[b], loc_out.at[b], out_sem.at[b]) for b in range(2)]
    out_copies[0].start()
    ring_forward(1)
    to_dev, to_gain = obs_order(1)
    band_statistics(1)
    ring_finish(1)
    out_copies[1].start()
    all_statistics(1, to_dev, to_gain)

    for b in range(2):
        for copy in ring[b]:
            copy.wait_send()
        for k in range(1, n_slab):
            a_copy(b, k).wait_send()
        for k in range(1, n_lev):
            b_copy(b, k).wait_send()
    for copy in out_copies:
        copy.wait()


def exchange(chunks, n_slab, n_lev, obs_cell, obs_value, obs_var, obs_frac, loc_level, ensemble, loc_column):
    members, lev_rows, cols = ensemble.shape
    n_obs = obs_cell.shape[1]
    held = loc_column.shape[1]
    vmem = pl.BlockSpec(memory_space=pltpu.VMEM)
    hbm = pl.BlockSpec(memory_space=pl.ANY)
    dma = pltpu.SemaphoreType.DMA
    return pl.pallas_call(
        functools.partial(exchange_kernel, chunks, n_slab, n_lev),
        out_shape=(
            jax.ShapeDtypeStruct((2, n_lev, held, cols), BF16),
            jax.ShapeDtypeStruct((2, n_obs, members), BF16),
            jax.ShapeDtypeStruct((2, members, n_obs), BF16),
            jax.ShapeDtypeStruct((2, n_obs), F32),
        ),
        in_specs=[vmem] * 5 + [hbm] * 2,
        out_specs=(hbm, vmem, vmem, vmem),
        scratch_shapes=[
            pltpu.VMEM((lev_rows, members, cols), F32),
            pltpu.VMEM((2, n_lev, held, cols), BF16),
            pltpu.VMEM((2, n_slab, chunks, members // 2, 128), F32),
            pltpu.VMEM((2, n_lev, chunks, members + 16, 128), BF16),
            pltpu.VMEM((3 * members, 256 * chunks), F32),
            dma((lev_rows,)),
            dma((2,)),
            dma((2,)),
            dma((2, n_slab)),
            dma((2, n_slab)),
            dma((2, n_lev)),
            dma((2, n_lev)),
            dma((2, 10)),
            dma((2, 10)),
        ],
        compiler_params=pltpu.CompilerParams(
            collective_id=chunks, has_side_effects=True, vmem_limit_bytes=60 * 1024 * 1024
        ),
    )(obs_cell, obs_value, obs_var, obs_frac, loc_level, ensemble, loc_column)


def regress_kernel(
    width, dev_ref, gain_ref, level_ref, ens_hbm, loc_hbm, out_hbm,
    ens, out, loc, level, in_sem, loc_sem, out_sem,
):
    lev_rows, members, cols = ens.shape
    n_obs = dev_ref.shape[1]
    steps = cols // width

    def at(c):
        return pl.ds(pl.multiple_of(c * width, width), width)

    def in_copy(c, l):
        return pltpu.make_async_copy(ens_hbm.at[:, l, at(c)], ens.at[l, :, at(c)], in_sem.at[c, l])

    def loc_copy(c, b):
        return pltpu.make_async_copy(loc_hbm.at[b, :, at(c)], loc.at[b, :, at(c)], loc_sem.at[c, b])

    def out_copy(c, l):
        return pltpu.make_async_copy(out.at[l, :, at(c)], out_hbm.at[:, l, at(c)], out_sem.at[c, l])

    for c in range(steps):
        for b in range(2):
            loc_copy(c, b).start()
        for l in range(lev_rows):
            in_copy(c, l).start()
    for b in range(2):
        for l in range(lev_rows):
            level[b, l] = jnp.broadcast_to(level_ref[b, :, l : l + 1], (n_obs, 128))

    def step(c, carry):
        for b in range(2):
            loc_copy(c, b).wait()
        for l in range(lev_rows):
            in_copy(c, l).wait()
        for b in range(2):
            source = ens if b == 0 else out
            local = loc[b, :, at(c)].astype(F32)
            for l in range(lev_rows):
                now = source[l, :, at(c)]
                mean = jnp.sum(now, axis=0, keepdims=True) / float(members)
                centred = (now - mean).astype(BF16)
                cross = jnp.dot(dev_ref[b], centred, preferred_element_type=F32)
                weight = jnp.tile(level[b, l], (1, width // 128)) * local
                mixed = (weight * cross).astype(BF16)
                out[l, :, at(c)] = now + jnp.dot(gain_ref[b], mixed, preferred_element_type=F32)
        for l in range(lev_rows):
            out_copy(c, l).start()
        return carry

    lax.fori_loop(0, steps, step, 0)
    for c in range(steps):
        for l in range(lev_rows):
            out_copy(c, l).wait()


def regress(dev, gain, loc_level, ensemble, loc_all):
    members, lev_rows, cols = ensemble.shape
    n_obs = dev.shape[1]
    width = 768 if cols % 768 == 0 else cols
    vmem = pl.BlockSpec(memory_space=pltpu.VMEM)
    hbm = pl.BlockSpec(memory_space=pl.ANY)
    dma = pltpu.SemaphoreType.DMA
    return pl.pallas_call(
        functools.partial(regress_kernel, width),
        out_shape=jax.ShapeDtypeStruct(ensemble.shape, F32),
        in_specs=[vmem] * 3 + [hbm] * 2,
        out_specs=hbm,
        scratch_shapes=[
            pltpu.VMEM((lev_rows, members, cols), F32),
            pltpu.VMEM((lev_rows, members, cols), F32),
            pltpu.VMEM((2, n_obs, cols), BF16),
            pltpu.VMEM((2, lev_rows, n_obs, 128), F32),
            dma((cols // width, lev_rows)),
            dma((cols // width, 2)),
            dma((cols // width, lev_rows)),
        ],
        compiler_params=pltpu.CompilerParams(vmem_limit_bytes=60 * 1024 * 1024),
    )(dev, gain, loc_level, ensemble, loc_all)


def on_device(n_slab, n_lev, ensemble, obs_cell, obs_value, obs_var, obs_frac, loc_column, loc_level):
    members, lev_rows, slab_cols = ensemble.shape
    n_obs = obs_cell.shape[1]
    band = obs_cell // (slab_cols * n_slab * lev_rows)
    crowd = jnp.sum((band[:, :, None] == jnp.arange(n_lev)).astype(jnp.int32), axis=1)
    operands = (obs_cell, obs_value, obs_var, obs_frac, loc_level, ensemble, loc_column)
    loc_all, dev, gain, prior_mean = lax.cond(
        jnp.max(crowd) <= SLOTS,
        functools.partial(exchange, 1, n_slab, n_lev),
        functools.partial(exchange, 3, n_slab, n_lev),
        *operands,
    )
    analysis = regress(dev, gain, loc_level, ensemble, loc_all.reshape(2, n_obs, slab_cols))
    return analysis, prior_mean


def solution(mesh):
    in_specs = (
        P(None, "lev", "slab"),
        P(),
        P(),
        P(),
        P(),
        P(None, "lev", "slab"),
        P(None, None, "lev"),
    )
    out_specs = (P(None, "lev", "slab"), P())
    return jax.shard_map(
        functools.partial(on_device, mesh.shape["slab"], mesh.shape["lev"]),
        mesh=mesh, in_specs=in_specs, out_specs=out_specs, check_vma=False,
    )
```

time: 269 us -> 53.8 us (0.20)
  waiting for transfers between devices: 150 us -> 0 us
  Pallas kernels: 0 us -> 46.8 us
  local copies, waits for them, and re-layouts: 48.4 us -> 3.67 us
  other arithmetic: 31.1 us -> 1.48 us
  matrix products: 16.3 us -> 0 us
  between operations: 14.6 us -> 1.3 us
  starting transfers between devices: 7.07 us -> 0 us
    psum x1 -> x0, waiting for transfers between devices: 150 us -> none  [on_device(): summed = lax.psum(tuple(pieces), ('slab', 'lev'))]
    pallas_call x0 -> x2, Pallas kernels: none -> 46.8 us  [the longest x1 36.5 us: exchange(): pl.pallas_call(functools.partial(exchange_kernel, chunks, n_slab, n_lev),...]
    gather x10 -> x0, local copies, waits for them, and re-layouts: 21.6 us -> none  [the longest x4 14.8 us: cell_values(): picked = jnp.take(flattened, row_safe * slab_cols + col_safe, axis=1)]
    dot_general x18 -> x0, matrix products: 16.3 us -> none  [the longest x8 7.74 us: regress_rows(): jnp.dot(gain_rows.T, mixed_rows, preferred_element_type=jnp.float32)]
    reshape x10 -> x0, local copies, waits for them, and re-layouts: 9.82 us -> none  [the longest x2 9.15 us: on_device(): current = current + increment.reshape(members, lev_rows, slab_cols)]
    unnamed x60 -> x2, local copies, waits for them, and re-layouts: 10.4 us -> 2.12 us
    all_to_all x1 -> x0, starting transfers between devices: 7.07 us -> none  [sent_to_all(): return lax.all_to_all(copies, axis, split_axis=0, concat_axis=0, tiled=True)]
    reduce_sum x7 -> x1, other arithmetic: 6.95 us -> 0.14 us  [on_device(): jnp.sum((band[:, :, None] == jnp.arange(n_lev)).astype(jnp.int32), axis=1)]
  transfers between devices with their start and end apart: 2 -> 0, of which waited for: 1 -> 0; matrix products, arithmetic and copies ran while one was open for 21% -> 0% of each run, Pallas kernels for 0% -> 0%
where the time goes in v1:
time: 53.8 us; the launch traced here: 53.5 us
  Pallas kernels  46.8 us (87%)
  local copies, waits for them, and re-layouts  3.67 us (7%)
  other arithmetic  1.48 us (3%)
  between operations  1.3 us (2%)
    pallas_call x1, Pallas kernels, exchange(): pl.pallas_call(functools.partial(exchange_kernel, chunks, n_slab, n_lev),...  36.5 us
    pallas_call x1, Pallas kernels, regress(): pl.pallas_call(functools.partial(regress_kernel, width), out_shape=jax.Sh...  10.3 us
    unnamed x2, local copies, waits for them, and re-layouts  2.12 us
    another operation x1, local copies, waits for them, and re-layouts  1.55 us

profile of v1, /device:TPU:1, one launch (start us, length us, event | category | flops | bytes accessed | tf_op | source)
XLA Modules:
  0.0 53.5 jit_solution(18191378441874501301)
XLA Ops:
  0.6 0.7 %and_select_fusion = s32[2,256]{1,0:T(2,128)S(1)} fusion(s32[2,256]{1,0:T(2,128)} %param.10), kind=kLoop, calls=%fused_computation.2 | loop fusion | flops 4096 | bytes 4096 | tf_op jit(solution)/shard_map/jit(floor_divide)/jit(_where)/select_n | solution.py:459
  1.3 0.1 convert_reduce_fusion
  1.5 0.6 %reduce_max.9 = s32[]{:T(128)} reduce(s32[2,8]{1,0:T(2,128)S(1)} %convert_reduce_fusion, s32[]{:T(128)} %constant.14.clone.1), dimensions={0,1}, to_apply=%region_1.2 | reduce | flops 15 | bytes 72 | tf_op jit(solution)/shard_map/reduce_max | solution.py:463
  2.8 1.5 %copy.14.level_ref = f32[2,256,4]{2,1,0:T(8,128)} copy(f32[2,256,4]{1,2,0:T(4,128)} %param.15) | data formatting | bytes 16384 | tf_op args[6]
  4.3 38.3 %conditional.1 = ((bf16[2,8,32,2304]{3,2,1,0:T(8,128)(2,1)S(1)}, bf16[2,256,80]{2,1,0:T(8,128)(2,1)S(1)}, bf16[2,80,256]{2,1,0:T(8,128)(2,1)S(1)}, f32[2,256]{1,0:T(2,128)S(1)})) conditional(s32[]{:T(128)} %convert_element_type.7, (s32[2,256]{1,0:T(2,128)}, f32[2,256]{1,0:T(2,128)}, f32[2,256]{1,0:T(2,128)}, f32[2,256]{1,0:T(2,128)}, ...), branch_computations={%region_2.3_spmd, %region_3.4_spmd} | conditional | bytes 16392 | solution.py:462
  4.3 1.5 %copy.13.level_ref = f32[2,256,4]{2,1,0:T(8,128)} copy(f32[2,256,4]{1,2,0:T(4,128)} %get-tuple-element.100) | data formatting | bytes 16384 | tf_op jit(solution)/shard_map
  5.9 36.5 %branch_1_fun.1 = (bf16[2,8,32,2304]{3,2,1,0:T(8,128)(2,1)S(1)}, bf16[2,256,80]{2,1,0:T(8,128)(2,1)S(1)}, bf16[2,80,256]{2,1,0:T(8,128)(2,1)S(1)}, f32[2,256]{1,0:T(2,128)S(1)}) custom-call(s32[2,256]{1,0:T(2,128)} %get-tuple-element.49.cell_ref, f32[2,256]{1,0:T(2,128)} %get-tuple-element.50.value_ref, f32[2,256]{1,0:T(2,128)} %get-tuple-element.51.var_ref, ...), custom_call_target="tpu_custom_call" | custom-call | tf_op jit(solution)/shard_map/cond/branch_1_fun/pallas_call | solution.py:344
  42.6 10.3 %shard_map.86 = f32[80,4,2304]{2,1,0:T(4,128)} custom-call(bf16[2,256,80]{2,1,0:T(8,128)(2,1)S(1)} %get-tuple-element.107.dev_ref, bf16[2,80,256]{2,1,0:T(8,128)(2,1)S(1)} %get-tuple-element.106.gain_ref, f32[2,256,4]{2,1,0:T(8,128)} %copy.14.level_ref, f32[80,4,2304]{2,1,0:T(4,128)} %ens_hbm.1, bf16[2,256,2304]{2,1,0:T(8,128)(2,1)S(1)} %bitcast.1), custom_call_target="tpu_custom_call" | custom-call | tf_op jit(solution)/shard_map/pallas_call | solution.py:438
  52.9 0.6 %copy.24 = f32[2,256]{1,0:T(2,128)} copy(f32[2,256]{1,0:T(2,128)S(1)} %get-tuple-element.121) | data formatting | bytes 4096

commit v2 on v1

--- a/solution.py
+++ b/solution.py
@@ -32,31 +32,58 @@
     return high, mid, low
 
 
-def exchange_kernel(
-    chunks, n_slab, n_lev,
-    cell_ref, value_ref, var_ref, frac_ref, level_ref, ens_hbm, loc_hbm,
-    loc_out, dev_out, gain_out, mean_out,
-    ens, loc, abuf, bbuf, acc,
-    ens_sem, own_sem, out_sem, a_send, a_recv, b_send, b_recv, l_send, l_recv,
+class Tracker:
+    def __init__(self):
+        self.sends = []
+        self.recvs = []
+
+    def start(self, copy):
+        copy.start()
+        self.sends.append(copy)
+        self.recvs.append(copy)
+
+    def arrived(self, copy):
+        copy.wait_recv()
+        self.recvs = [c for c in self.recvs if c is not copy]
+
+    def drain(self):
+        for copy in self.recvs:
+            copy.wait_recv()
+        for copy in self.sends:
+            copy.wait_send()
+
+
+def filter_kernel(
+    chunks, n_slab, n_lev, width,
+    cell_hbm, value_hbm, var_hbm, frac_hbm, level_hbm, ens_hbm, loc_hbm,
+    ens, loc_last, dev_out, gain_out, level_out, mean_out,
+    loc_first, cell_ref, value_ref, var_ref, frac_ref, level_ref, abuf, bbuf, acc, level_wide,
+    small_sem, ens_sem, own_sem, a_send, a_recv, b_send, b_recv, l_send, l_recv,
 ):
     slab = lax.axis_index("slab")
     lev = lax.axis_index("lev")
     lev_rows, members, cols = ens.shape
     n_obs = cell_ref.shape[1]
+    loc = (loc_first, loc_last)
     total_cols = cols * n_slab
     half = members // 2
+    remote = Tracker()
 
     barrier = pltpu.get_barrier_semaphore()
     slab_peer = [lax.rem(slab + k, n_slab) for k in range(n_slab)]
     lev_peer = [lax.rem(lev + k, n_lev) for k in range(n_lev)]
+    for k in range(1, n_slab):
+        pl.semaphore_signal(barrier, inc=1, device_id=(slab_peer[k], lev), device_id_type=MESH)
     for k in range(1, n_lev):
         pl.semaphore_signal(barrier, inc=1, device_id=(slab, lev_peer[k]), device_id_type=MESH)
-    for k in range(1, n_slab):
-        pl.semaphore_signal(barrier, inc=1, device_id=(slab_peer[k], lev), device_id_type=MESH)
-    own_copies = [
-        pltpu.make_async_copy(loc_hbm.at[b], loc.at[b, lev], own_sem.at[b]) for b in range(2)
+    small_copies = [
+        pltpu.make_async_copy(source, target, small_sem.at[i])
+        for i, (source, target) in enumerate([
+            (cell_hbm, cell_ref), (value_hbm, value_ref), (var_hbm, var_ref),
+            (frac_hbm, frac_ref), (level_hbm, level_ref),
+        ])
     ]
-    for copy in own_copies:
+    for copy in small_copies:
         copy.start()
     ens_copies = [
         pltpu.make_async_copy(ens_hbm.at[:, l, :], ens.at[l], ens_sem.at[l])
@@ -64,6 +91,14 @@
     ]
     for copy in ens_copies:
         copy.start()
+    own_copies = [
+        pltpu.make_async_copy(loc_hbm.at[b], loc[b].at[lev], own_sem.at[b]) for b in range(2)
+    ]
+    for copy in own_copies:
+        copy.start()
+
+    for copy in small_copies:
+        copy.wait()
 
     slab_f = slab.astype(F32)
     lev_f = lev.astype(F32)
@@ -84,12 +119,14 @@
         rows.append(
             [band, places[0], places[1], inner,
              value_ref[pl.ds(b, 1), :], var_ref[pl.ds(b, 1), :], frac_ref[pl.ds(b, 1), :]]
-        )
+            + [level_ref[b, pl.ds(l, 1), :] for l in range(lev_rows)]
+        )
+    per_block = len(rows[0])
     flat = rows[0] + rows[1]
     table = jnp.concatenate(flat + [jnp.zeros((128 - len(flat), n_obs), F32)], axis=0).T
 
     def column_of(b, i):
-        return table[:, 7 * b + i : 7 * b + i + 1]
+        return table[:, per_block * b + i : per_block * b + i + 1]
 
     lane = lax.broadcasted_iota(jnp.int32, (n_obs, 128), 1)
     lane_slot = jnp.where(lane < SLOTS, lane, lane - SLOTS).astype(F32)
@@ -120,7 +157,7 @@
         slot_info.append(per_chunk)
 
     def loc_copy(b, which, holder, start, count, target):
-        piece = loc.at[b, holder, pl.ds(start, count)]
+        piece = loc[b].at[holder, pl.ds(start, count)]
         return pltpu.make_async_remote_copy(
             src_ref=piece, dst_ref=piece,
             send_sem=l_send.at[b, which], recv_sem=l_recv.at[b, which],
@@ -131,7 +168,7 @@
     down = lax.rem(lev + n_lev - 2, n_lev)
     far = lax.rem(lev + 4, n_lev)
     mate = lev + 1 - 2 * lax.rem(lev, 2)
-    held = loc.shape[2]
+    held = loc_first.shape[1]
     part = held // 2
     ring = []
     for b in range(2):
@@ -150,38 +187,32 @@
 
     def ring_begin(b):
         for i in (0, 1, 2, 3, 6):
-            ring[b][i].start()
+            remote.start(ring[b][i])
 
     def ring_forward(b):
-        ring[b][0].wait_recv()
-        ring[b][4].start()
-        ring[b][1].wait_recv()
-        ring[b][5].start()
-        ring[b][2].wait_recv()
-        ring[b][7].start()
-        ring[b][3].wait_recv()
-        ring[b][8].start()
+        for first, then in ((0, 4), (1, 5), (2, 7), (3, 8)):
+            remote.arrived(ring[b][first])
+            remote.start(ring[b][then])
 
     def ring_finish(b):
-        ring[b][4].wait_recv()
-        ring[b][5].wait_recv()
-        ring[b][9].start()
+        remote.arrived(ring[b][4])
+        remote.arrived(ring[b][5])
+        remote.start(ring[b][9])
         for i in (6, 7, 8, 9):
-            ring[b][i].wait_recv()
-
-    def a_copy(r, k):
-        return pltpu.make_async_remote_copy(
+            remote.arrived(ring[b][i])
+
+    a_copies = [[
+        pltpu.make_async_remote_copy(
             src_ref=abuf.at[r, 0], dst_ref=abuf.at[r, k],
             send_sem=a_send.at[r, k], recv_sem=a_recv.at[r, k],
             device_id=(slab_peer[k], lev), device_id_type=MESH,
-        )
-
-    def b_copy(r, k):
-        return pltpu.make_async_remote_copy(
+        ) if k else None for k in range(n_slab)] for r in range(2)]
+    b_copies = [[
+        pltpu.make_async_remote_copy(
             src_ref=bbuf.at[r, 0], dst_ref=bbuf.at[r, k],
             send_sem=b_send.at[r, k], recv_sem=b_recv.at[r, k],
             device_id=(slab, lev_peer[k]), device_id_type=MESH,
-        )
+        ) if k else None for k in range(n_lev)] for r in range(2)]
 
     lane1 = lax.broadcasted_iota(jnp.int32, (1, 128), 1)
     low1 = lane1 < SLOTS
@@ -192,11 +223,11 @@
             both = weighted + pltpu.roll(weighted, SLOTS, 1)
             abuf[r, 0, q] = jnp.where(low1, both[:half], both[half:])
         for k in range(1, n_slab):
-            a_copy(r, k).start()
+            remote.start(a_copies[r][k])
 
     def band_statistics(r):
         for k in range(1, n_slab):
-            a_copy(r, k).wait_recv()
+            remote.arrived(a_copies[r][k])
         for q in range(chunks):
             packed = abuf[r, 0, q]
             for k in range(1, n_slab):
@@ -218,7 +249,7 @@
             parts = jnp.where(row == 0, high, jnp.where(row == 1, mid, jnp.where(row == 2, low, 0.0)))
             bbuf[r, 0, q, pl.ds(members, 16), :] = parts.astype(BF16)
         for k in range(1, n_lev):
-            b_copy(r, k).start()
+            remote.start(b_copies[r][k])
 
     def obs_order(r):
         away = lev_f - column_of(r, 0)
@@ -234,17 +265,38 @@
 
     def all_statistics(r, to_dev, to_gain):
         for k in range(1, n_lev):
-            b_copy(r, k).wait_recv()
+            remote.arrived(b_copies[r][k])
         packed = jnp.concatenate(
             [bbuf[r, k, q] for k in range(n_lev) for q in range(chunks)], axis=1
         )
         dev = nt_dot(to_dev, packed)[:, :members].astype(BF16)
         gain = nt_dot(packed[:members], to_gain).astype(BF16)
-        means = nt_dot(packed[members:], to_dev)
-        dev_out[r] = dev
-        gain_out[r] = gain
+        return dev, gain
+
+    def all_means(r, to_dev):
+        packed = jnp.concatenate(
+            [bbuf[r, k, q, pl.ds(members, 16), :] for k in range(n_lev) for q in range(chunks)], axis=1
+        )
+        means = nt_dot(packed, to_dev)
         mean_out[pl.ds(r, 1), :] = means[0:1] + means[1:2] + means[2:3]
-        return dev, gain
+
+    def at(c):
+        return pl.ds(pl.multiple_of(c * width, width), width)
+
+    def regress(dev, gain):
+        def step(c, carry):
+            local = loc_first[:, :, at(c)].reshape(n_obs, width).astype(F32)
+            for l in range(lev_rows):
+                now = ens[l, :, at(c)]
+                mean = jnp.sum(now, axis=0, keepdims=True) / float(members)
+                centred = (now - mean).astype(BF16)
+                cross = jnp.dot(dev, centred, preferred_element_type=F32)
+                weight = jnp.tile(level_wide[l], (1, width // 128)) * local
+                mixed = (weight * cross).astype(BF16)
+                ens[l, :, at(c)] = now + jnp.dot(gain, mixed, preferred_element_type=F32)
+            return carry
+
+        lax.fori_loop(0, cols // width, step, 0)
 
     wide = 256 * chunks
     places = jnp.concatenate(
@@ -255,10 +307,6 @@
     )
     at_level = [jnp.where(inners == float(l), places, -1.0) for l in range(lev_rows)]
     acc[...] = jnp.zeros_like(acc)
-
-    pl.semaphore_wait(barrier, n_lev + n_slab - 2)
-    own_copies[0].wait()
-    ring_begin(0)
     for copy in ens_copies:
         copy.wait()
 
@@ -287,10 +335,16 @@
         for b in range(2)
     ]
 
+    pl.semaphore_wait(barrier, n_lev + n_slab - 2)
     send_priors(0, cells[0])
+    own_copies[0].wait()
+    ring_begin(0)
+    to_dev, to_gain = obs_order(0)
+    for l in range(lev_rows):
+        level_wide[l] = jnp.broadcast_to(column_of(0, 7 + l), (n_obs, 128))
+    level_out[...] = table
     ring_forward(0)
     own_copies[1].wait()
-    to_dev, to_gain = obs_order(0)
     band_statistics(0)
     ring_finish(0)
 
@@ -299,10 +353,10 @@
     narrow = 128 * chunks
     index = lax.broadcasted_iota(jnp.int32, (cols, narrow), 0).astype(F32)
     hot = jnp.where(index == later_places, 1.0, 0.0).astype(BF16)
-    weights = jnp.dot(loc[0].reshape(n_obs, cols), hot, preferred_element_type=F32)
+    weights = jnp.dot(loc_first[...].reshape(n_obs, cols), hot, preferred_element_type=F32)
     level_weight = jnp.zeros((n_obs, narrow), F32)
     for l in range(lev_rows):
-        level_weight = jnp.where(later_inners == float(l), level_ref[0, :, l : l + 1], level_weight)
+        level_weight = jnp.where(later_inners == float(l), column_of(0, 7 + l), level_weight)
     weights = level_weight * weights
 
     dev, gain = all_statistics(0, to_dev, to_gain)
@@ -313,52 +367,52 @@
     mixed = (weights * cross).astype(BF16)
     now = now + jnp.dot(gain, mixed, preferred_element_type=F32)
     send_priors(1, [now[:, 128 * q : 128 * (q + 1)] for q in range(chunks)])
-
-    out_copies = [pltpu.make_async_copy(loc.at[b], loc_out.at[b], out_sem.at[b]) for b in range(2)]
-    out_copies[0].start()
+    all_means(0, to_dev)
+    regress(dev, gain)
     ring_forward(1)
     to_dev, to_gain = obs_order(1)
     band_statistics(1)
     ring_finish(1)
-    out_copies[1].start()
-    all_statistics(1, to_dev, to_gain)
-
-    for b in range(2):
-        for copy in ring[b]:
-            copy.wait_send()
-        for k in range(1, n_slab):
-            a_copy(b, k).wait_send()
-        for k in range(1, n_lev):
-            b_copy(b, k).wait_send()
-    for copy in out_copies:
-        copy.wait()
-
-
-def exchange(chunks, n_slab, n_lev, obs_cell, obs_value, obs_var, obs_frac, loc_level, ensemble, loc_column):
+    dev, gain = all_statistics(1, to_dev, to_gain)
+    dev_out[...] = dev
+    gain_out[...] = gain
+    all_means(1, to_dev)
+    remote.drain()
+
+
+def run_filter(chunks, n_slab, n_lev, obs_cell, obs_value, obs_var, obs_frac, loc_level, ensemble, loc_column):
     members, lev_rows, cols = ensemble.shape
     n_obs = obs_cell.shape[1]
     held = loc_column.shape[1]
+    width = 768 if cols % 768 == 0 else cols
     vmem = pl.BlockSpec(memory_space=pltpu.VMEM)
-    hbm = pl.BlockSpec(memory_space=pl.ANY)
+    hbm = pl.BlockSpec(memory_space=pltpu.HBM)
     dma = pltpu.SemaphoreType.DMA
     return pl.pallas_call(
-        functools.partial(exchange_kernel, chunks, n_slab, n_lev),
+        functools.partial(filter_kernel, chunks, n_slab, n_lev, width),
         out_shape=(
-            jax.ShapeDtypeStruct((2, n_lev, held, cols), BF16),
-            jax.ShapeDtypeStruct((2, n_obs, members), BF16),
-            jax.ShapeDtypeStruct((2, members, n_obs), BF16),
+            jax.ShapeDtypeStruct((lev_rows, members, cols), F32),
+            jax.ShapeDtypeStruct((n_lev, held, cols), BF16),
+            jax.ShapeDtypeStruct((n_obs, members), BF16),
+            jax.ShapeDtypeStruct((members, n_obs), BF16),
+            jax.ShapeDtypeStruct((n_obs, 128), F32),
             jax.ShapeDtypeStruct((2, n_obs), F32),
         ),
-        in_specs=[vmem] * 5 + [hbm] * 2,
-        out_specs=(hbm, vmem, vmem, vmem),
+        in_specs=[hbm] * 7,
+        out_specs=(vmem,) * 6,
         scratch_shapes=[
-            pltpu.VMEM((lev_rows, members, cols), F32),
-            pltpu.VMEM((2, n_lev, held, cols), BF16),
+            pltpu.VMEM((n_lev, held, cols), BF16),
+            pltpu.VMEM(obs_cell.shape, jnp.int32),
+            pltpu.VMEM(obs_cell.shape, F32),
+            pltpu.VMEM(obs_cell.shape, F32),
+            pltpu.VMEM(obs_cell.shape, F32),
+            pltpu.VMEM(loc_level.shape, F32),
             pltpu.VMEM((2, n_slab, chunks, members // 2, 128), F32),
             pltpu.VMEM((2, n_lev, chunks, members + 16, 128), BF16),
             pltpu.VMEM((3 * members, 256 * chunks), F32),
+            pltpu.VMEM((lev_rows, n_obs, 128), F32),
+            dma((5,)),
             dma((lev_rows,)),
-            dma((2,)),
             dma((2,)),
             dma((2, n_slab)),
             dma((2, n_slab)),
@@ -368,57 +422,35 @@
             dma((2, 10)),
         ],
         compiler_params=pltpu.CompilerParams(
-            collective_id=chunks, has_side_effects=True, vmem_limit_bytes=60 * 1024 * 1024
+            collective_id=chunks, has_side_effects=True, vmem_limit_bytes=VMEM_LIMIT
         ),
     )(obs_cell, obs_value, obs_var, obs_frac, loc_level, ensemble, loc_column)
 
 
-def regress_kernel(
-    width, dev_ref, gain_ref, level_ref, ens_hbm, loc_hbm, out_hbm,
-    ens, out, loc, level, in_sem, loc_sem, out_sem,
-):
+def last_kernel(width, ens, loc, dev_ref, gain_ref, level_ref, out_hbm, out, out_sem):
     lev_rows, members, cols = ens.shape
-    n_obs = dev_ref.shape[1]
+    n_obs = dev_ref.shape[0]
     steps = cols // width
 
     def at(c):
         return pl.ds(pl.multiple_of(c * width, width), width)
 
-    def in_copy(c, l):
-        return pltpu.make_async_copy(ens_hbm.at[:, l, at(c)], ens.at[l, :, at(c)], in_sem.at[c, l])
-
-    def loc_copy(c, b):
-        return pltpu.make_async_copy(loc_hbm.at[b, :, at(c)], loc.at[b, :, at(c)], loc_sem.at[c, b])
-
     def out_copy(c, l):
         return pltpu.make_async_copy(out.at[l, :, at(c)], out_hbm.at[:, l, at(c)], out_sem.at[c, l])
 
-    for c in range(steps):
-        for b in range(2):
-            loc_copy(c, b).start()
+    dev = dev_ref[...]
+    gain = gain_ref[...]
+
+    def step(c, carry):
+        local = loc[:, :, at(c)].reshape(n_obs, width).astype(F32)
         for l in range(lev_rows):
-            in_copy(c, l).start()
-    for b in range(2):
-        for l in range(lev_rows):
-            level[b, l] = jnp.broadcast_to(level_ref[b, :, l : l + 1], (n_obs, 128))
-
-    def step(c, carry):
-        for b in range(2):
-            loc_copy(c, b).wait()
-        for l in range(lev_rows):
-            in_copy(c, l).wait()
-        for b in range(2):
-            source = ens if b == 0 else out
-            local = loc[b, :, at(c)].astype(F32)
-            for l in range(lev_rows):
-                now = source[l, :, at(c)]
-                mean = jnp.sum(now, axis=0, keepdims=True) / float(members)
-                centred = (now - mean).astype(BF16)
-                cross = jnp.dot(dev_ref[b], centred, preferred_element_type=F32)
-                weight = jnp.tile(level[b, l], (1, width // 128)) * local
-                mixed = (weight * cross).astype(BF16)
-                out[l, :, at(c)] = now + jnp.dot(gain_ref[b], mixed, preferred_element_type=F32)
-        for l in range(lev_rows):
+            now = ens[l, :, at(c)]
+            mean = jnp.sum(now, axis=0, keepdims=True) / float(members)
+            centred = (now - mean).astype(BF16)
+            cross = jnp.dot(dev, centred, preferred_element_type=F32)
+            place = LEVEL_AT + l
+            mixed = (level_ref[:, place : place + 1] * local * cross).astype(BF16)
+            out[l, :, at(c)] = now + jnp.dot(gain, mixed, preferred_element_type=F32)
             out_copy(c, l).start()
         return carry
 
@@ -428,45 +460,47 @@
             out_copy(c, l).wait()
 
 
-def regress(dev, gain, loc_level, ensemble, loc_all):
-    members, lev_rows, cols = ensemble.shape
-    n_obs = dev.shape[1]
+LEVEL_AT = 18
+VMEM_LIMIT = 40 * 1024 * 1024
+COND = True
+
+
+def last_update(ens, loc, dev, gain, level):
+    lev_rows, members, cols = ens.shape
     width = 768 if cols % 768 == 0 else cols
     vmem = pl.BlockSpec(memory_space=pltpu.VMEM)
-    hbm = pl.BlockSpec(memory_space=pl.ANY)
-    dma = pltpu.SemaphoreType.DMA
     return pl.pallas_call(
-        functools.partial(regress_kernel, width),
-        out_shape=jax.ShapeDtypeStruct(ensemble.shape, F32),
-        in_specs=[vmem] * 3 + [hbm] * 2,
-        out_specs=hbm,
+        functools.partial(last_kernel, width),
+        out_shape=jax.ShapeDtypeStruct((members, lev_rows, cols), F32),
+        in_specs=[vmem] * 5,
+        out_specs=pl.BlockSpec(memory_space=pl.ANY),
         scratch_shapes=[
             pltpu.VMEM((lev_rows, members, cols), F32),
-            pltpu.VMEM((lev_rows, members, cols), F32),
-            pltpu.VMEM((2, n_obs, cols), BF16),
-            pltpu.VMEM((2, lev_rows, n_obs, 128), F32),
-            dma((cols // width, lev_rows)),
-            dma((cols // width, 2)),
-            dma((cols // width, lev_rows)),
+            pltpu.SemaphoreType.DMA((cols // width, lev_rows)),
         ],
-        compiler_params=pltpu.CompilerParams(vmem_limit_bytes=60 * 1024 * 1024),
-    )(dev, gain, loc_level, ensemble, loc_all)
+        compiler_params=pltpu.CompilerParams(vmem_limit_bytes=VMEM_LIMIT),
+    )(ens, loc, dev, gain, level)
 
 
 def on_device(n_slab, n_lev, ensemble, obs_cell, obs_value, obs_var, obs_frac, loc_column, loc_level):
     members, lev_rows, slab_cols = ensemble.shape
     n_obs = obs_cell.shape[1]
-    band = obs_cell // (slab_cols * n_slab * lev_rows)
-    crowd = jnp.sum((band[:, :, None] == jnp.arange(n_lev)).astype(jnp.int32), axis=1)
-    operands = (obs_cell, obs_value, obs_var, obs_frac, loc_level, ensemble, loc_column)
-    loc_all, dev, gain, prior_mean = lax.cond(
-        jnp.max(crowd) <= SLOTS,
-        functools.partial(exchange, 1, n_slab, n_lev),
-        functools.partial(exchange, 3, n_slab, n_lev),
-        *operands,
-    )
-    analysis = regress(dev, gain, loc_level, ensemble, loc_all.reshape(2, n_obs, slab_cols))
-    return analysis, prior_mean
+    operands = (obs_cell, obs_value, obs_var, obs_frac, jnp.swapaxes(loc_level, 1, 2), ensemble, loc_column)
+    if COND:
+        band_cells = slab_cols * n_slab * lev_rows
+        starts = jnp.arange(n_lev, dtype=jnp.int32) * band_cells
+        cell = obs_cell[:, :, None]
+        inside = (cell >= starts) & (cell < starts + band_cells)
+        crowd = jnp.max(jnp.sum(inside.astype(jnp.int32), axis=1))
+        state = lax.cond(
+            crowd <= SLOTS,
+            functools.partial(run_filter, 1, n_slab, n_lev),
+            functools.partial(run_filter, 3, n_slab, n_lev),
+            *operands,
+        )
+    else:
+        state = run_filter(1, n_slab, n_lev, *operands)
+    return last_update(*state[:5]), state[5]
 
 
 def solution(mesh):

time: 53.8 us -> 47.6 us (0.88)
  Pallas kernels: 46.8 us -> 43.7 us
  local copies, waits for them, and re-layouts: 3.67 us -> 0.58 us
    pallas_call x2, Pallas kernels: 46.8 us -> 43.7 us  [the longest x1 36.3 us: run_filter(): pl.pallas_call(functools.partial(filter_kernel, chunks, n_slab, n_lev, wi...]
    another operation x1 -> x0, local copies, waits for them, and re-layouts: 1.55 us -> none
    unnamed x2 -> x1, local copies, waits for them, and re-layouts: 2.12 us -> 0.58 us
    reduce_sum x1, other arithmetic: 0.14 us -> 0.89 us  [on_device(): crowd = jnp.max(jnp.sum(inside.astype(jnp.int32), axis=1))]
    select_n x1 -> x0, other arithmetic: 0.69 us -> none  [on_device(): band = obs_cell // (slab_cols * n_slab * lev_rows)]
where the time goes in v2:
time: 47.6 us; the launch traced here: 47.4 us
  Pallas kernels  43.7 us (92%)
  other arithmetic  1.54 us (3%)
  between operations  1.31 us (3%)
  local copies, waits for them, and re-layouts  0.58 us (1%)
    pallas_call x1, Pallas kernels, run_filter(): pl.pallas_call(functools.partial(filter_kernel, chunks, n_slab, n_lev, wi...  36.3 us
    pallas_call x1, Pallas kernels, last_update(): pl.pallas_call(functools.partial(last_kernel, width), out_shape=jax.Shape...  7.39 us

profile of v2, /device:TPU:1, one launch (start us, length us, event | category | flops | bytes accessed | tf_op | source)
XLA Modules:
  0.0 47.4 jit_solution(1063592833046130410)
XLA Ops:
  0.6 0.9 %convert_reduce_fusion = s32[2,8]{1,0:T(2,128)S(1)} fusion(s32[2,256]{1,0:T(2,128)} %param.10, s32[8]{0:T(128)S(1)} %get-tuple-element.57, s32[8]{0:T(128)S(1)} %get-tuple-element.56), kind=kLoop, calls=%fused_computation | loop fusion | flops 20464 | bytes 2176 | tf_op jit(solution)/shard_map/reduce_sum | solution.py:494
  1.5 0.6 %reduce_max.9 = s32[]{:T(128)} reduce(s32[2,8]{1,0:T(2,128)S(1)} %convert_reduce_fusion, s32[]{:T(128)} %constant.2.clone.1), dimensions={0,1}, to_apply=%region_1.0 | reduce | flops 15 | bytes 72 | tf_op jit(solution)/shard_map/reduce_max | solution.py:494
  2.8 36.5 %conditional.1 = ((f32[4,80,2304]{2,1,0:T(8,128)S(1)}, bf16[8,32,2304]{2,1,0:T(8,128)(2,1)}, bf16[256,80]{1,0:T(8,128)(2,1)S(1)}, bf16[80,256]{1,0:T(8,128)(2,1)...) conditional(s32[]{:T(128)} %convert_element_type.7, (s32[2,256]{1,0:T(2,128)}, f32[2,256]{1,0:T(2,128)}, ...), branch_computations={%region_2.0_spmd, %region_3.0_spmd} | conditional | bytes 8 | solution.py:495
  3.0 36.3 %branch_1_fun.1 = (f32[4,80,2304]{2,1,0:T(8,128)S(1)}, bf16[8,32,2304]{2,1,0:T(8,128)(2,1)}, bf16[256,80]{1,0:T(8,128)(2,1)S(1)}, bf16[80,256]{1,0:T(8,128)(2,1)...) custom-call(s32[2,256]{1,0:T(2,128)} %get-tuple-element.35.cell_hbm, f32[2,256]{1,0:T(2,128)} %get-tuple-element.36.value_hbm, ...), custom_call_target="tpu_custom_call" | custom-call | tf_op jit(solution)/shard_map/cond/branch_1_fun/pallas_call | solution.py:391
  39.4 7.4 %shard_map.86 = f32[80,4,2304]{2,1,0:T(4,128)} custom-call(f32[4,80,2304]{2,1,0:T(8,128)S(1)} %get-tuple-element.50.ens, bf16[8,32,2304]{2,1,0:T(8,128)(2,1)} %get-tuple-element.51.loc, bf16[256,80]{1,0:T(8,128)(2,1)S(1)} %get-tuple-element.52.dev_ref, bf16[80,256]{1,0:T(8,128)(2,1)S(1)} %get-tuple-element.53.gain_ref, ...), custom_call_target="tpu_custom_call" | custom-call | tf_op jit(solution)/shard_map/pallas_call | solution.py:472
  46.8 0.6 %copy.22 = f32[2,256]{1,0:T(2,128)} copy(f32[2,256]{1,0:T(2,128)S(1)} %get-tuple-element.73) | data formatting | bytes 4096
  (1 shorter events, 0.0 us)

commit v3 on v2

--- a/solution.py
+++ b/solution.py
@@ -384,7 +384,7 @@
     members, lev_rows, cols = ensemble.shape
     n_obs = obs_cell.shape[1]
     held = loc_column.shape[1]
-    width = 768 if cols % 768 == 0 else cols
+    width = WIDTH if cols % WIDTH == 0 else cols
     vmem = pl.BlockSpec(memory_space=pltpu.VMEM)
     hbm = pl.BlockSpec(memory_space=pltpu.HBM)
     dma = pltpu.SemaphoreType.DMA
@@ -427,56 +427,44 @@
     )(obs_cell, obs_value, obs_var, obs_frac, loc_level, ensemble, loc_column)
 
 
-def last_kernel(width, ens, loc, dev_ref, gain_ref, level_ref, out_hbm, out, out_sem):
+def last_kernel(ens, loc, dev_ref, gain_ref, level_ref, out_hbm, out, out_sem):
     lev_rows, members, cols = ens.shape
     n_obs = dev_ref.shape[0]
-    steps = cols // width
-
-    def at(c):
-        return pl.ds(pl.multiple_of(c * width, width), width)
-
-    def out_copy(c, l):
-        return pltpu.make_async_copy(out.at[l, :, at(c)], out_hbm.at[:, l, at(c)], out_sem.at[c, l])
-
     dev = dev_ref[...]
     gain = gain_ref[...]
-
-    def step(c, carry):
-        local = loc[:, :, at(c)].reshape(n_obs, width).astype(F32)
-        for l in range(lev_rows):
-            now = ens[l, :, at(c)]
-            mean = jnp.sum(now, axis=0, keepdims=True) / float(members)
-            centred = (now - mean).astype(BF16)
-            cross = jnp.dot(dev, centred, preferred_element_type=F32)
-            place = LEVEL_AT + l
-            mixed = (level_ref[:, place : place + 1] * local * cross).astype(BF16)
-            out[l, :, at(c)] = now + jnp.dot(gain, mixed, preferred_element_type=F32)
-            out_copy(c, l).start()
-        return carry
-
-    lax.fori_loop(0, steps, step, 0)
-    for c in range(steps):
-        for l in range(lev_rows):
-            out_copy(c, l).wait()
+    copies = []
+    for l in range(lev_rows):
+        now = ens[l]
+        mean = jnp.sum(now, axis=0, keepdims=True) / float(members)
+        centred = (now - mean).astype(BF16)
+        cross = jnp.dot(dev, centred, preferred_element_type=F32)
+        place = LEVEL_AT + l
+        weight = level_ref[:, place : place + 1] * loc[...].reshape(n_obs, cols).astype(F32)
+        mixed = (weight * cross).astype(BF16)
+        out[l] = now + jnp.dot(gain, mixed, preferred_element_type=F32)
+        copies.append(pltpu.make_async_copy(out.at[l], out_hbm.at[:, l, :], out_sem.at[l]))
+        copies[l].start()
+    for copy in copies:
+        copy.wait()
 
 
 LEVEL_AT = 18
 VMEM_LIMIT = 40 * 1024 * 1024
+WIDTH = 2304
 COND = True
 
 
 def last_update(ens, loc, dev, gain, level):
     lev_rows, members, cols = ens.shape
-    width = 768 if cols % 768 == 0 else cols
     vmem = pl.BlockSpec(memory_space=pltpu.VMEM)
     return pl.pallas_call(
-        functools.partial(last_kernel, width),
-        out_shape=jax.ShapeDtypeStruct((members, lev_rows, cols), F32),
+        last_kernel,
+        out_shape=pltpu.HBM((members, lev_rows, cols), F32),
         in_specs=[vmem] * 5,
-        out_specs=pl.BlockSpec(memory_space=pl.ANY),
+        out_specs=pl.BlockSpec(memory_space=pltpu.HBM),
         scratch_shapes=[
             pltpu.VMEM((lev_rows, members, cols), F32),
-            pltpu.SemaphoreType.DMA((cols // width, lev_rows)),
+            pltpu.SemaphoreType.DMA((lev_rows,)),
         ],
         compiler_params=pltpu.CompilerParams(vmem_limit_bytes=VMEM_LIMIT),
     )(ens, loc, dev, gain, level)
@@ -486,21 +474,21 @@
     members, lev_rows, slab_cols = ensemble.shape
     n_obs = obs_cell.shape[1]
     operands = (obs_cell, obs_value, obs_var, obs_frac, jnp.swapaxes(loc_level, 1, 2), ensemble, loc_column)
-    if COND:
-        band_cells = slab_cols * n_slab * lev_rows
-        starts = jnp.arange(n_lev, dtype=jnp.int32) * band_cells
-        cell = obs_cell[:, :, None]
-        inside = (cell >= starts) & (cell < starts + band_cells)
-        crowd = jnp.max(jnp.sum(inside.astype(jnp.int32), axis=1))
-        state = lax.cond(
-            crowd <= SLOTS,
-            functools.partial(run_filter, 1, n_slab, n_lev),
-            functools.partial(run_filter, 3, n_slab, n_lev),
-            *operands,
-        )
-    else:
-        state = run_filter(1, n_slab, n_lev, *operands)
-    return last_update(*state[:5]), state[5]
+
+    def whole(chunks, *arrays):
+        state = run_filter(chunks, n_slab, n_lev, *arrays)
+        return last_update(*state[:5]), state[5]
+
+    if not COND:
+        return whole(1, *operands)
+    band_cells = slab_cols * n_slab * lev_rows
+    starts = jnp.arange(n_lev, dtype=jnp.int32) * band_cells
+    cell = obs_cell[:, :, None]
+    inside = (cell >= starts) & (cell < starts + band_cells)
+    crowd = jnp.max(jnp.sum(inside.astype(jnp.int32), axis=1))
+    return lax.cond(
+        crowd <= SLOTS, functools.partial(whole, 1), functools.partial(whole, 3), *operands
+    )
 
 
 def solution(mesh):

time: 47.6 us -> 43.1 us (0.905)
  Pallas kernels: 43.7 us -> 39.3 us
    pallas_call x1, Pallas kernels: 7.39 us -> 3.69 us  [last_update(): pl.pallas_call(last_kernel, out_shape=pltpu.HBM((members, lev_rows, cols)...]
    pallas_call x1, Pallas kernels: 36.3 us -> 35.6 us  [run_filter(): pl.pallas_call(functools.partial(filter_kernel, chunks, n_slab, n_lev, wi...]
where the time goes in v3:
time: 43.1 us; the launch traced here: 42.9 us
  Pallas kernels  39.3 us (91%)
  other arithmetic  1.54 us (4%)
  between operations  1.3 us (3%)
  local copies, waits for them, and re-layouts  0.58 us (1%)
    pallas_call x1, Pallas kernels, run_filter(): pl.pallas_call(functools.partial(filter_kernel, chunks, n_slab, n_lev, wi...  35.6 us
    pallas_call x1, Pallas kernels, last_update(): pl.pallas_call(last_kernel, out_shape=pltpu.HBM((members, lev_rows, cols)...  3.69 us
    reduce_sum x1, other arithmetic, on_device(): crowd = jnp.max(jnp.sum(inside.astype(jnp.int32), axis=1))  0.89 us

profile of v3, /device:TPU:1, one launch (start us, length us, event | category | flops | bytes accessed | tf_op | source)
XLA Modules:
  0.0 42.9 jit_solution(17643844231800468358)
XLA Ops:
  0.6 0.9 %convert_reduce_fusion = s32[2,8]{1,0:T(2,128)S(1)} fusion(s32[2,256]{1,0:T(2,128)} %param.10, s32[8]{0:T(128)S(1)} %get-tuple-element.78, s32[8]{0:T(128)S(1)} %get-tuple-element.77), kind=kLoop, calls=%fused_computation | loop fusion | flops 20464 | bytes 2176 | tf_op jit(solution)/shard_map/reduce_sum | solution.py:488
  1.5 0.6 %reduce_max.9 = s32[]{:T(128)} reduce(s32[2,8]{1,0:T(2,128)S(1)} %convert_reduce_fusion, s32[]{:T(128)} %constant.2.clone.1), dimensions={0,1}, to_apply=%region_1.0 | reduce | flops 15 | bytes 72 | tf_op jit(solution)/shard_map/reduce_max | solution.py:488
  2.8 39.5 %conditional.1 = (f32[2,256]{1,0:T(2,128)S(1)}, f32[80,4,2304]{2,1,0:T(4,128)}) conditional(s32[]{:T(128)} %convert_element_type.7, (s32[2,256]{1,0:T(2,128)}, f32[2,256]{1,0:T(2,128)}, f32[2,256]{1,0:T(2,128)}, f32[2,256]{1,0:T(2,128)}, f32[2,4,256]{2,1,0:T(4,128)}, /*index=5*/f32[80,4,2304]{2,1,0:T(4,128)}, ...), branch_computations={%region_2.0_spmd, %region_3.0_spmd} | conditional | bytes 16 | solution.py:489
  3.0 35.6 %branch_1_fun.2 = (f32[4,80,2304]{2,1,0:T(8,128)S(1)}, bf16[8,32,2304]{2,1,0:T(8,128)(2,1)S(1)}, bf16[256,80]{1,0:T(8,128)(2,1)S(1)}, bf16[80,256]{1,0:T(8,128)(...) custom-call(s32[2,256]{1,0:T(2,128)} %get-tuple-element.41.cell_hbm, f32[2,256]{1,0:T(2,128)} %get-tuple-element.68.value_hbm, ...), custom_call_target="tpu_custom_call" | custom-call | tf_op jit(solution)/shard_map/cond/branch_1_fun/pallas_call | solution.py:391
  38.6 3.7 %branch_1_fun.3 = f32[80,4,2304]{2,1,0:T(4,128)} custom-call(f32[4,80,2304]{2,1,0:T(8,128)S(1)} %get-tuple-element.48.ens, bf16[8,32,2304]{2,1,0:T(8,128)(2,1)S(1)} %get-tuple-element.49.loc, bf16[256,80]{1,0:T(8,128)(2,1)S(1)} %get-tuple-element.50.dev_ref, bf16[80,256]{1,0:T(8,128)(2,1)S(1)} %get-tuple-element.51.gain_ref, ...), custom_call_target="tpu_custom_call" | custom-call | tf_op jit(solution)/shard_map/cond/branch_1_fun/pallas_call | solution.py:460
  42.3 0.6 %copy.26 = f32[2,256]{1,0:T(2,128)} copy(f32[2,256]{1,0:T(2,128)S(1)} %get-tuple-element.86) | data formatting | bytes 4096
  (1 shorter events, 0.0 us)

commit v4 on v3

--- a/solution.py
+++ b/solution.py
@@ -56,8 +56,8 @@
 def filter_kernel(
     chunks, n_slab, n_lev, width,
     cell_hbm, value_hbm, var_hbm, frac_hbm, level_hbm, ens_hbm, loc_hbm,
-    ens, loc_last, dev_out, gain_out, level_out, mean_out,
-    loc_first, cell_ref, value_ref, var_ref, frac_ref, level_ref, abuf, bbuf, acc, level_wide,
+    ens, loc_last, dev_out, gain_out, level_out, mean_out, crowd_out,
+    loc_first, cell_ref, value_ref, var_ref, frac_ref, level_ref, abuf, bbuf, level_wide,
     small_sem, ens_sem, own_sem, a_send, a_recv, b_send, b_recv, l_send, l_recv,
 ):
     slab = lax.axis_index("slab")
@@ -102,8 +102,11 @@
 
     slab_f = slab.astype(F32)
     lev_f = lev.astype(F32)
-    rows = []
-    for b in range(2):
+    lane = lax.broadcasted_iota(jnp.int32, (n_obs, 128), 1)
+    lane_slot = jnp.where(lane < SLOTS, lane, lane - SLOTS).astype(F32)
+    first_half = lane < SLOTS
+
+    def locate(b):
         cell = cell_ref[pl.ds(b, 1), :].astype(F32)
         level = count_at_least(cell, total_cols, n_lev * lev_rows)
         column = cell - level * float(total_cols)
@@ -116,45 +119,56 @@
             in_slab = count_at_least(where_at, cols, n_slab)
             place = where_at - in_slab * float(cols) + 1.0
             places.append(jnp.where(in_slab == slab_f, place, 0.0))
-        rows.append(
-            [band, places[0], places[1], inner,
-             value_ref[pl.ds(b, 1), :], var_ref[pl.ds(b, 1), :], frac_ref[pl.ds(b, 1), :]]
-            + [level_ref[b, pl.ds(l, 1), :] for l in range(lev_rows)]
-        )
-    per_block = len(rows[0])
-    flat = rows[0] + rows[1]
-    table = jnp.concatenate(flat + [jnp.zeros((128 - len(flat), n_obs), F32)], axis=0).T
-
-    def column_of(b, i):
-        return table[:, per_block * b + i : per_block * b + i + 1]
-
-    lane = lax.broadcasted_iota(jnp.int32, (n_obs, 128), 1)
-    lane_slot = jnp.where(lane < SLOTS, lane, lane - SLOTS).astype(F32)
-    first_half = lane < SLOTS
-    ranks = []
-    slot_info = []
-    for b in range(2):
+        flat = [band, places[0], places[1], inner,
+                value_ref[pl.ds(b, 1), :], var_ref[pl.ds(b, 1), :], frac_ref[pl.ds(b, 1), :]]
+        flat = flat + [level_ref[b, pl.ds(l, 1), :] for l in range(lev_rows)]
+        table = jnp.concatenate(flat + [jnp.zeros((128 - len(flat), n_obs), F32)], axis=0).T
         other = lax.broadcasted_iota(jnp.int32, (n_obs, n_obs), 1)
         mine = lax.broadcasted_iota(jnp.int32, (n_obs, n_obs), 0)
-        earlier = (column_of(b, 0) == rows[b][0]) & (other < mine)
+        earlier = (table[:, 0:1] == band) & (other < mine)
         rank = jnp.sum(jnp.where(earlier, 1.0, 0.0), axis=1, keepdims=True)
-        ranks.append(rank)
-        per_chunk = []
+        return table, rank, jnp.max(rank)
+
+    def column_of(found, i):
+        return found[0][:, i : i + 1]
+
+    def picked(found, q, x):
+        chosen = (column_of(found, 0) == lev_f) & (found[1] == lane_slot + float(SLOTS * q))
+        return jnp.sum(jnp.where(chosen, x, 0.0), axis=0, keepdims=True)
+
+    def slot_places(found):
+        place = jnp.where(first_half, column_of(found, 1), column_of(found, 2))
+        inner = jnp.broadcast_to(column_of(found, 3), (n_obs, 128))
+        return (
+            jnp.concatenate([picked(found, q, place) - 1.0 for q in range(chunks)], axis=1),
+            jnp.concatenate([picked(found, q, inner) for q in range(chunks)], axis=1),
+        )
+
+    def slot_weights(found):
+        frac = column_of(found, 6)
+        weight = jnp.where(first_half, 1.0 - frac, frac)
+        return [picked(found, q, weight) for q in range(chunks)]
+
+    def slot_values(found):
+        pairs = []
         for q in range(chunks):
-            chosen = (column_of(b, 0) == lev_f) & (rank == lane_slot + float(SLOTS * q))
-
-            def picked(x):
-                return jnp.sum(jnp.where(chosen, x, 0.0), axis=0, keepdims=True)
-
-            filled = picked(jnp.ones((n_obs, 128), F32))
-            place = picked(jnp.where(first_half, column_of(b, 1), column_of(b, 2))) - 1.0
-            inner = picked(jnp.broadcast_to(column_of(b, 3), (n_obs, 128)))
-            value = picked(jnp.broadcast_to(column_of(b, 4), (n_obs, 128)))
-            var = picked(jnp.broadcast_to(column_of(b, 5), (n_obs, 128))) + (1.0 - filled)
-            frac = column_of(b, 6)
-            weight = picked(jnp.where(first_half, 1.0 - frac, frac))
-            per_chunk.append((place, inner, value, var, weight))
-        slot_info.append(per_chunk)
+            value = picked(found, q, column_of(found, 4))
+            var = picked(found, q, column_of(found, 5) - 1.0) + 1.0
+            pairs.append((value, var))
+        return pairs
+
+    def gather_cells(places, inners):
+        index = lax.broadcasted_iota(jnp.int32, (cols, 128 * chunks), 0).astype(F32)
+        hot = jnp.where(index == places, 1.0, 0.0).astype(BF16)
+        cells = jnp.zeros((members, 128 * chunks), F32)
+        for l in range(lev_rows):
+            left = jnp.concatenate(split3(ens[l])[:PIECES], axis=0)
+            found = jnp.dot(left, hot, preferred_element_type=F32)
+            total = found[:members]
+            for i in range(1, PIECES):
+                total = total + found[i * members : (i + 1) * members]
+            cells = jnp.where(inners == float(l), total, cells)
+        return hot, jnp.where(places >= 0.0, cells, 0.0)
 
     def loc_copy(b, which, holder, start, count, target):
         piece = loc[b].at[holder, pl.ds(start, count)]
@@ -217,15 +231,15 @@
     lane1 = lax.broadcasted_iota(jnp.int32, (1, 128), 1)
     low1 = lane1 < SLOTS
 
-    def send_priors(r, cells):
+    def send_priors(r, cells, weights):
         for q in range(chunks):
-            weighted = cells[q] * slot_info[r][q][4]
+            weighted = cells[:, 128 * q : 128 * (q + 1)] * weights[q]
             both = weighted + pltpu.roll(weighted, SLOTS, 1)
             abuf[r, 0, q] = jnp.where(low1, both[:half], both[half:])
         for k in range(1, n_slab):
             remote.start(a_copies[r][k])
 
-    def band_statistics(r):
+    def band_statistics(r, values):
         for k in range(1, n_slab):
             remote.arrived(a_copies[r][k])
         for q in range(chunks):
@@ -236,7 +250,7 @@
             prior = jnp.concatenate(
                 [jnp.where(low1, packed, turned), jnp.where(low1, turned, packed)], axis=0
             )
-            _, _, value, variance, _ = slot_info[r][q]
+            value, variance = values[q]
             mean = jnp.sum(prior, axis=0, keepdims=True) / float(members)
             deviation = prior - mean
             spread = jnp.sum(deviation * deviation, axis=0, keepdims=True) / (members - 1.0)
@@ -251,14 +265,14 @@
         for k in range(1, n_lev):
             remote.start(b_copies[r][k])
 
-    def obs_order(r):
-        away = lev_f - column_of(r, 0)
+    def obs_order(found):
+        away = lev_f - column_of(found, 0)
         away = jnp.where(away < 0.0, away + float(n_lev), away)
         to_dev = []
         to_gain = []
         for k in range(n_lev):
             for q in range(chunks):
-                chosen = (away == float(k)) & (ranks[r] == lane_slot + float(SLOTS * q))
+                chosen = (away == float(k)) & (found[1] == lane_slot + float(SLOTS * q))
                 to_dev.append(jnp.where(chosen & first_half, 1.0, 0.0).astype(BF16))
                 to_gain.append(jnp.where(chosen & ~first_half, 1.0, 0.0).astype(BF16))
         return jnp.concatenate(to_dev, axis=1), jnp.concatenate(to_gain, axis=1)
@@ -298,80 +312,52 @@
 
         lax.fori_loop(0, cols // width, step, 0)
 
-    wide = 256 * chunks
-    places = jnp.concatenate(
-        [slot_info[b][q][0] for b in range(2) for q in range(chunks)], axis=1
-    )
-    inners = jnp.concatenate(
-        [slot_info[b][q][1] for b in range(2) for q in range(chunks)], axis=1
-    )
-    at_level = [jnp.where(inners == float(l), places, -1.0) for l in range(lev_rows)]
-    acc[...] = jnp.zeros_like(acc)
+    found0 = locate(0)
+    places, inners = slot_places(found0)
+    weights0 = slot_weights(found0)
     for copy in ens_copies:
         copy.wait()
-
-    step_cols = 256
-
-    def gather_step(c, carry):
-        base = c * step_cols
-        here = pl.ds(pl.multiple_of(base, step_cols), step_cols)
-        index = (lax.broadcasted_iota(jnp.int32, (step_cols, wide), 0) + base).astype(F32)
-        hot = jnp.concatenate(
-            [jnp.where(index == at_level[l], 1.0, 0.0).astype(BF16) for l in range(lev_rows)],
-            axis=0,
-        )
-        pieces = [split3(ens[l, :, here]) for l in range(lev_rows)]
-        left = jnp.concatenate(
-            [jnp.concatenate([pieces[l][i] for l in range(lev_rows)], axis=1) for i in range(3)],
-            axis=0,
-        )
-        acc[...] += jnp.dot(left, hot, preferred_element_type=F32)
-        return carry
-
-    lax.fori_loop(0, cols // step_cols, gather_step, 0)
-    picked_cells = acc[:members] + acc[members : 2 * members] + acc[2 * members :]
-    cells = [
-        [picked_cells[:, 128 * (b * chunks + q) : 128 * (b * chunks + q + 1)] for q in range(chunks)]
-        for b in range(2)
-    ]
-
+    _, cells = gather_cells(places, inners)
     pl.semaphore_wait(barrier, n_lev + n_slab - 2)
-    send_priors(0, cells[0])
+    send_priors(0, cells, weights0)
     own_copies[0].wait()
     ring_begin(0)
-    to_dev, to_gain = obs_order(0)
-    for l in range(lev_rows):
-        level_wide[l] = jnp.broadcast_to(column_of(0, 7 + l), (n_obs, 128))
-    level_out[...] = table
+
+    values0 = slot_values(found0)
+    found1 = locate(1)
+    places, inners = slot_places(found1)
+    weights1 = slot_weights(found1)
+    hot, now = gather_cells(places, inners)
+    to_dev, to_gain = obs_order(found0)
     ring_forward(0)
     own_copies[1].wait()
-    band_statistics(0)
+    band_statistics(0, values0)
+    for l in range(lev_rows):
+        level_wide[l] = jnp.broadcast_to(column_of(found0, 7 + l), (n_obs, 128))
+    level_out[...] = found1[0]
     ring_finish(0)
 
-    later_places = jnp.concatenate([slot_info[1][q][0] for q in range(chunks)], axis=1)
-    later_inners = jnp.concatenate([slot_info[1][q][1] for q in range(chunks)], axis=1)
-    narrow = 128 * chunks
-    index = lax.broadcasted_iota(jnp.int32, (cols, narrow), 0).astype(F32)
-    hot = jnp.where(index == later_places, 1.0, 0.0).astype(BF16)
     weights = jnp.dot(loc_first[...].reshape(n_obs, cols), hot, preferred_element_type=F32)
-    level_weight = jnp.zeros((n_obs, narrow), F32)
+    level_weight = jnp.zeros((n_obs, 128 * chunks), F32)
     for l in range(lev_rows):
-        level_weight = jnp.where(later_inners == float(l), column_of(0, 7 + l), level_weight)
+        level_weight = jnp.where(inners == float(l), column_of(found0, 7 + l), level_weight)
     weights = level_weight * weights
+    centred = (now - jnp.sum(now, axis=0, keepdims=True) / float(members)).astype(BF16)
 
     dev, gain = all_statistics(0, to_dev, to_gain)
-    ring_begin(1)
-    now = jnp.concatenate(cells[1], axis=1)
-    centred = (now - jnp.sum(now, axis=0, keepdims=True) / float(members)).astype(BF16)
     cross = jnp.dot(dev, centred, preferred_element_type=F32)
     mixed = (weights * cross).astype(BF16)
     now = now + jnp.dot(gain, mixed, preferred_element_type=F32)
-    send_priors(1, [now[:, 128 * q : 128 * (q + 1)] for q in range(chunks)])
+    send_priors(1, now, weights1)
+    ring_begin(1)
+
+    crowd_out[0] = (jnp.maximum(found0[2], found1[2]) >= float(SLOTS * chunks)).astype(jnp.int32)
     all_means(0, to_dev)
+    values1 = slot_values(found1)
     regress(dev, gain)
+    to_dev, to_gain = obs_order(found1)
     ring_forward(1)
-    to_dev, to_gain = obs_order(1)
-    band_statistics(1)
+    band_statistics(1, values1)
     ring_finish(1)
     dev, gain = all_statistics(1, to_dev, to_gain)
     dev_out[...] = dev
@@ -391,15 +377,16 @@
     return pl.pallas_call(
         functools.partial(filter_kernel, chunks, n_slab, n_lev, width),
         out_shape=(
-            jax.ShapeDtypeStruct((lev_rows, members, cols), F32),
-            jax.ShapeDtypeStruct((n_lev, held, cols), BF16),
-            jax.ShapeDtypeStruct((n_obs, members), BF16),
-            jax.ShapeDtypeStruct((members, n_obs), BF16),
-            jax.ShapeDtypeStruct((n_obs, 128), F32),
-            jax.ShapeDtypeStruct((2, n_obs), F32),
+            pltpu.VMEM((lev_rows, members, cols), F32),
+            pltpu.VMEM((n_lev, held, cols), BF16),
+            pltpu.VMEM((n_obs, members), BF16),
+            pltpu.VMEM((members, n_obs), BF16),
+            pltpu.VMEM((n_obs, 128), F32),
+            pltpu.VMEM((2, n_obs), F32),
+            jax.ShapeDtypeStruct((1,), jnp.int32),
         ),
         in_specs=[hbm] * 7,
-        out_specs=(vmem,) * 6,
+        out_specs=(vmem,) * 6 + (pl.BlockSpec(memory_space=pltpu.SMEM),),
         scratch_shapes=[
             pltpu.VMEM((n_lev, held, cols), BF16),
             pltpu.VMEM(obs_cell.shape, jnp.int32),
@@ -409,7 +396,6 @@
             pltpu.VMEM(loc_level.shape, F32),
             pltpu.VMEM((2, n_slab, chunks, members // 2, 128), F32),
             pltpu.VMEM((2, n_lev, chunks, members + 16, 128), BF16),
-            pltpu.VMEM((3 * members, 256 * chunks), F32),
             pltpu.VMEM((lev_rows, n_obs, 128), F32),
             dma((5,)),
             dma((lev_rows,)),
@@ -424,15 +410,17 @@
         compiler_params=pltpu.CompilerParams(
             collective_id=chunks, has_side_effects=True, vmem_limit_bytes=VMEM_LIMIT
         ),
-    )(obs_cell, obs_value, obs_var, obs_frac, loc_level, ensemble, loc_column)
-
-
-def last_kernel(ens, loc, dev_ref, gain_ref, level_ref, out_hbm, out, out_sem):
+    )(*(pltpu.with_memory_space_constraint(x, pltpu.HBM) for x in (
+        obs_cell, obs_value, obs_var, obs_frac, loc_level, ensemble, loc_column)))
+
+
+def last_kernel(ens, loc, dev_ref, gain_ref, level_ref, mean_ref, out_hbm, mean_hbm, out, out_sem, mean_sem):
     lev_rows, members, cols = ens.shape
     n_obs = dev_ref.shape[0]
     dev = dev_ref[...]
     gain = gain_ref[...]
-    copies = []
+    copies = [pltpu.make_async_copy(mean_ref, mean_hbm, mean_sem)]
+    copies[0].start()
     for l in range(lev_rows):
         now = ens[l]
         mean = jnp.sum(now, axis=0, keepdims=True) / float(members)
@@ -443,31 +431,34 @@
         mixed = (weight * cross).astype(BF16)
         out[l] = now + jnp.dot(gain, mixed, preferred_element_type=F32)
         copies.append(pltpu.make_async_copy(out.at[l], out_hbm.at[:, l, :], out_sem.at[l]))
-        copies[l].start()
+        copies[l + 1].start()
     for copy in copies:
         copy.wait()
 
 
-LEVEL_AT = 18
+LEVEL_AT = 7
+PIECES = 3
 VMEM_LIMIT = 40 * 1024 * 1024
 WIDTH = 2304
 COND = True
 
 
-def last_update(ens, loc, dev, gain, level):
+def last_update(ens, loc, dev, gain, level, mean):
     lev_rows, members, cols = ens.shape
     vmem = pl.BlockSpec(memory_space=pltpu.VMEM)
+    hbm = pl.BlockSpec(memory_space=pltpu.HBM)
     return pl.pallas_call(
         last_kernel,
-        out_shape=pltpu.HBM((members, lev_rows, cols), F32),
-        in_specs=[vmem] * 5,
-        out_specs=pl.BlockSpec(memory_space=pltpu.HBM),
+        out_shape=(pltpu.HBM((members, lev_rows, cols), F32), pltpu.HBM(mean.shape, F32)),
+        in_specs=[vmem] * 6,
+        out_specs=(hbm, hbm),
         scratch_shapes=[
             pltpu.VMEM((lev_rows, members, cols), F32),
             pltpu.SemaphoreType.DMA((lev_rows,)),
+            pltpu.SemaphoreType.DMA,
         ],
         compiler_params=pltpu.CompilerParams(vmem_limit_bytes=VMEM_LIMIT),
-    )(ens, loc, dev, gain, level)
+    )(*(pltpu.with_memory_space_constraint(x, pltpu.VMEM) for x in (ens, loc, dev, gain, level, mean)))
 
 
 def on_device(n_slab, n_lev, ensemble, obs_cell, obs_value, obs_var, obs_frac, loc_column, loc_level):
@@ -475,20 +466,12 @@
     n_obs = obs_cell.shape[1]
     operands = (obs_cell, obs_value, obs_var, obs_frac, jnp.swapaxes(loc_level, 1, 2), ensemble, loc_column)
 
-    def whole(chunks, *arrays):
-        state = run_filter(chunks, n_slab, n_lev, *arrays)
-        return last_update(*state[:5]), state[5]
-
-    if not COND:
-        return whole(1, *operands)
-    band_cells = slab_cols * n_slab * lev_rows
-    starts = jnp.arange(n_lev, dtype=jnp.int32) * band_cells
-    cell = obs_cell[:, :, None]
-    inside = (cell >= starts) & (cell < starts + band_cells)
-    crowd = jnp.max(jnp.sum(inside.astype(jnp.int32), axis=1))
-    return lax.cond(
-        crowd <= SLOTS, functools.partial(whole, 1), functools.partial(whole, 3), *operands
-    )
+    def whole(chunks):
+        *state, crowd = run_filter(chunks, n_slab, n_lev, *operands)
+        return (crowd[0], *last_update(*state))
+
+    done = lax.while_loop(lambda state: state[0] != 0, lambda state: whole(3), whole(1))
+    return done[1], done[2]
 
 
 def solution(mesh):

time: 43.1 us -> 39.9 us (0.926)
  other arithmetic: 1.54 us -> 0 us
  Pallas kernels: 39.3 us -> 38.1 us
  loops' own time: 0.21 us -> 0.79 us
  local copies, waits for them, and re-layouts: 0.58 us -> 0 us
  between operations: 1.3 us -> 0.83 us
    pallas_call x1, Pallas kernels: 35.6 us -> 34.4 us  [run_filter(): pl.pallas_call(functools.partial(filter_kernel, chunks, n_slab, n_lev, wi...]
    reduce_sum x1 -> x0, other arithmetic: 0.89 us -> none  [on_device(): crowd = jnp.max(jnp.sum(inside.astype(jnp.int32), axis=1))]
    reduce_max x1 -> x0, other arithmetic: 0.65 us -> none  [on_device(): crowd = jnp.max(jnp.sum(inside.astype(jnp.int32), axis=1))]
    unnamed x1 -> x0, local copies, waits for them, and re-layouts: 0.58 us -> none
    another operation x1, loops' own time: 0.21 us -> 0.79 us  [on_device(): lax.while_loop(lambda state: state[0] != 0, lambda state: whole(3), whole...]
where the time goes in v4:
time: 39.9 us; the launch traced here: 39.8 us
  Pallas kernels  38.1 us (95%)
  between operations  0.83 us (2%)
  loops' own time  0.79 us (2%)
    pallas_call x1, Pallas kernels, run_filter(): pl.pallas_call(functools.partial(filter_kernel, chunks, n_slab, n_lev, wi...  34.4 us
    pallas_call x1, Pallas kernels, last_update(): pl.pallas_call(last_kernel, out_shape=(pltpu.HBM((members, lev_rows, cols...  3.74 us

profile of v4, /device:TPU:1, one launch (start us, length us, event | category | flops | bytes accessed | tf_op | source)
XLA Modules:
  0.0 39.8 jit_solution(10100409841451325851)
XLA Ops:
  0.6 34.4 %shard_map.86 = (f32[4,80,2304]{2,1,0:T(8,128)S(1)}, bf16[8,32,2304]{2,1,0:T(8,128)(2,1)S(1)}, bf16[256,80]{1,0:T(8,128)(2,1)S(1)}, bf16[80,256]{1,0:T(8,128)(2,...) custom-call(s32[2,256]{1,0:T(2,128)} %cell_hbm.1, f32[2,256]{1,0:T(2,128)} %value_hbm.1, ...), custom_call_target="tpu_custom_call" | custom-call | tf_op jit(solution)/shard_map/pallas_call | solution.py:377
  35.0 3.7 %shard_map.87 = (f32[80,4,2304]{2,1,0:T(4,128)}, f32[2,256]{1,0:T(2,128)}) custom-call(f32[4,80,2304]{2,1,0:T(8,128)S(1)} %get-tuple-element.71.ens, bf16[8,32,2304]{2,1,0:T(8,128)(2,1)S(1)} %get-tuple-element.72.loc, bf16[256,80]{1,0:T(8,128)(2,1)S(1)} %get-tuple-element.73.dev_ref, bf16[80,256]{1,0:T(8,128)(2,1)S(1)} %get-tuple-element.74.gain_ref, ...), custom_call_target="tpu_custom_call" | custom-call | tf_op jit(solution)/shard_map/pallas_call | solution.py:450
  38.8 0.8 %while.11 = (s32[]{:T(128)}, f32[80,4,2304]{2,1,0:T(4,128)}, f32[2,256]{1,0:T(2,128)}, s32[2,256]{1,0:T(2,128)}, f32[2,256]{1,0:T(2,128)}, /*index=5*/f32[2,256]...) while((s32[]{:T(128)}, f32[80,4,2304]{2,1,0:T(4,128)}, ...), condition=%region_1.0_spmd, body=%region_0.0_spmd | while | flops 1 | bytes 89 | solution.py:473

commit v5 on v4

--- a/solution.py
+++ b/solution.py
@@ -1,4 +1,5 @@
 import functools
+import math
 
 import jax
 import jax.numpy as jnp
@@ -70,11 +71,27 @@
     remote = Tracker()
 
     barrier = pltpu.get_barrier_semaphore()
-    slab_peer = [lax.rem(slab + k, n_slab) for k in range(n_slab)]
-    lev_peer = [lax.rem(lev + k, n_lev) for k in range(n_lev)]
-    for k in range(1, n_slab):
+    side = math.isqrt(n_slab)
+    stack = n_lev // 2
+
+    def around(k, n):
+        return min(k, n - k)
+
+    slab_peer = [
+        lax.rem(slab // side + k // side, side) * side + lax.rem(lax.rem(slab, side) + k % side, side)
+        for k in range(n_slab)
+    ]
+    core = lax.rem(lev, 2)
+    lev_peer = [
+        lax.rem(lev // 2 + k // 2, stack) * 2 + (1 - core if k % 2 else core) for k in range(n_lev)
+    ]
+    slab_order = sorted(
+        range(1, n_slab), key=lambda k: -around(k // side, side) - around(k % side, side)
+    )
+    lev_order = sorted(range(1, n_lev), key=lambda k: -around(k // 2, stack))
+    for k in slab_order:
         pl.semaphore_signal(barrier, inc=1, device_id=(slab_peer[k], lev), device_id_type=MESH)
-    for k in range(1, n_lev):
+    for k in lev_order:
         pl.semaphore_signal(barrier, inc=1, device_id=(slab, lev_peer[k]), device_id_type=MESH)
     small_copies = [
         pltpu.make_async_copy(source, target, small_sem.at[i])
@@ -236,7 +253,7 @@
             weighted = cells[:, 128 * q : 128 * (q + 1)] * weights[q]
             both = weighted + pltpu.roll(weighted, SLOTS, 1)
             abuf[r, 0, q] = jnp.where(low1, both[:half], both[half:])
-        for k in range(1, n_slab):
+        for k in slab_order:
             remote.start(a_copies[r][k])
 
     def band_statistics(r, values):
@@ -262,12 +279,16 @@
             row = lax.broadcasted_iota(jnp.int32, (16, 128), 0)
             parts = jnp.where(row == 0, high, jnp.where(row == 1, mid, jnp.where(row == 2, low, 0.0)))
             bbuf[r, 0, q, pl.ds(members, 16), :] = parts.astype(BF16)
-        for k in range(1, n_lev):
+        for k in lev_order:
             remote.start(b_copies[r][k])
 
     def obs_order(found):
-        away = lev_f - column_of(found, 0)
-        away = jnp.where(away < 0.0, away + float(n_lev), away)
+        band = column_of(found, 0)
+        band_stack = count_at_least(band, 2, stack)
+        band_core = band - 2.0 * band_stack
+        away = (lev // 2).astype(F32) - band_stack
+        away = jnp.where(away < 0.0, away + float(stack), away) * 2.0
+        away = away + jnp.where(band_core == core.astype(F32), 0.0, 1.0)
         to_dev = []
         to_gain = []
         for k in range(n_lev):
@@ -319,9 +340,9 @@
         copy.wait()
     _, cells = gather_cells(places, inners)
     pl.semaphore_wait(barrier, n_lev + n_slab - 2)
-    send_priors(0, cells, weights0)
     own_copies[0].wait()
     ring_begin(0)
+    send_priors(0, cells, weights0)
 
     values0 = slot_values(found0)
     found1 = locate(1)
@@ -383,7 +404,7 @@
             pltpu.VMEM((members, n_obs), BF16),
             pltpu.VMEM((n_obs, 128), F32),
             pltpu.VMEM((2, n_obs), F32),
-            jax.ShapeDtypeStruct((1,), jnp.int32),
+            pltpu.SMEM((1,), jnp.int32),
         ),
         in_specs=[hbm] * 7,
         out_specs=(vmem,) * 6 + (pl.BlockSpec(memory_space=pltpu.SMEM),),

time: 39.9 us -> 38.4 us (0.962)
  Pallas kernels: 38.1 us -> 37.2 us
  loops' own time: 0.79 us -> 0.23 us
    pallas_call x1, Pallas kernels: 34.4 us -> 33.5 us  [run_filter(): pl.pallas_call(functools.partial(filter_kernel, chunks, n_slab, n_lev, wi...]
    another operation x1, loops' own time: 0.79 us -> 0.23 us  [on_device(): lax.while_loop(lambda state: state[0] != 0, lambda state: whole(3), whole...]
where the time goes in v5:
time: 38.4 us; the launch traced here: 38.2 us
  Pallas kernels  37.2 us (97%)
  between operations  0.83 us (2%)
    pallas_call x1, Pallas kernels, run_filter(): pl.pallas_call(functools.partial(filter_kernel, chunks, n_slab, n_lev, wi...  33.5 us
    pallas_call x1, Pallas kernels, last_update(): pl.pallas_call(last_kernel, out_shape=(pltpu.HBM((members, lev_rows, cols...  3.73 us

profile of v5, /device:TPU:1, one launch (start us, length us, event | category | flops | bytes accessed | tf_op | source)
XLA Modules:
  0.0 38.2 jit_solution(5822381419600274164)
XLA Ops:
  0.6 33.5 %shard_map.86 = (f32[4,80,2304]{2,1,0:T(8,128)S(1)}, bf16[8,32,2304]{2,1,0:T(8,128)(2,1)S(1)}, bf16[256,80]{1,0:T(8,128)(2,1)S(1)}, bf16[80,256]{1,0:T(8,128)(2,...) custom-call(s32[2,256]{1,0:T(2,128)} %cell_hbm.1, f32[2,256]{1,0:T(2,128)} %value_hbm.1, ...), custom_call_target="tpu_custom_call" | custom-call | tf_op jit(solution)/shard_map/pallas_call | solution.py:398
  34.1 3.7 %shard_map.87 = (f32[80,4,2304]{2,1,0:T(4,128)}, f32[2,256]{1,0:T(2,128)}) custom-call(f32[4,80,2304]{2,1,0:T(8,128)S(1)} %get-tuple-element.71.ens, bf16[8,32,2304]{2,1,0:T(8,128)(2,1)S(1)} %get-tuple-element.72.loc, bf16[256,80]{1,0:T(8,128)(2,1)S(1)} %get-tuple-element.73.dev_ref, bf16[80,256]{1,0:T(8,128)(2,1)S(1)} %get-tuple-element.74.gain_ref, ...), custom_call_target="tpu_custom_call" | custom-call | tf_op jit(solution)/shard_map/pallas_call | solution.py:471
  37.8 0.2 while.11

commit v6 on v5

--- a/solution.py
+++ b/solution.py
@@ -18,6 +18,11 @@
     return lax.dot_general(a, b, (((1,), (1,)), ((), ())), preferred_element_type=F32)
 
 
+def mean_of(packed, to_dev):
+    parts = nt_dot(packed, to_dev)
+    return parts[0:1] + parts[1:2] + parts[2:3]
+
+
 def count_at_least(x, step, number):
     total = jnp.zeros_like(x)
     for k in range(1, number):
@@ -57,8 +62,8 @@
 def filter_kernel(
     chunks, n_slab, n_lev, width,
     cell_hbm, value_hbm, var_hbm, frac_hbm, level_hbm, ens_hbm, loc_hbm,
-    ens, loc_last, dev_out, gain_out, level_out, mean_out, crowd_out,
-    loc_first, cell_ref, value_ref, var_ref, frac_ref, level_ref, abuf, bbuf, level_wide,
+    ens, centred_out, weight_out, dev_out, gain_out, place_out, packed_out, mean_out, crowd_out,
+    loc_first, loc_last, cell_ref, value_ref, var_ref, frac_ref, level_ref, abuf, bbuf, level_wide,
     small_sem, ens_sem, own_sem, a_send, a_recv, b_send, b_recv, l_send, l_recv,
 ):
     slab = lax.axis_index("slab")
@@ -308,12 +313,10 @@
         gain = nt_dot(packed[:members], to_gain).astype(BF16)
         return dev, gain
 
-    def all_means(r, to_dev):
-        packed = jnp.concatenate(
+    def mean_rows(r):
+        return jnp.concatenate(
             [bbuf[r, k, q, pl.ds(members, 16), :] for k in range(n_lev) for q in range(chunks)], axis=1
         )
-        means = nt_dot(packed, to_dev)
-        mean_out[pl.ds(r, 1), :] = means[0:1] + means[1:2] + means[2:3]
 
     def at(c):
         return pl.ds(pl.multiple_of(c * width, width), width)
@@ -328,7 +331,10 @@
                 cross = jnp.dot(dev, centred, preferred_element_type=F32)
                 weight = jnp.tile(level_wide[l], (1, width // 128)) * local
                 mixed = (weight * cross).astype(BF16)
-                ens[l, :, at(c)] = now + jnp.dot(gain, mixed, preferred_element_type=F32)
+                now = now + jnp.dot(gain, mixed, preferred_element_type=F32)
+                ens[l, :, at(c)] = now
+                mean = jnp.sum(now, axis=0, keepdims=True) / float(members)
+                centred_out[l, :, at(c)] = (now - mean).astype(BF16)
             return carry
 
         lax.fori_loop(0, cols // width, step, 0)
@@ -355,7 +361,6 @@
     band_statistics(0, values0)
     for l in range(lev_rows):
         level_wide[l] = jnp.broadcast_to(column_of(found0, 7 + l), (n_obs, 128))
-    level_out[...] = found1[0]
     ring_finish(0)
 
     weights = jnp.dot(loc_first[...].reshape(n_obs, cols), hot, preferred_element_type=F32)
@@ -373,17 +378,21 @@
     ring_begin(1)
 
     crowd_out[0] = (jnp.maximum(found0[2], found1[2]) >= float(SLOTS * chunks)).astype(jnp.int32)
-    all_means(0, to_dev)
+    mean_out[...] = mean_of(mean_rows(0), to_dev)
     values1 = slot_values(found1)
     regress(dev, gain)
     to_dev, to_gain = obs_order(found1)
+    place_out[...] = to_dev
     ring_forward(1)
     band_statistics(1, values1)
     ring_finish(1)
+    local = loc_last[...].reshape(n_obs, cols).astype(F32)
+    for l in range(lev_rows):
+        weight_out[l] = column_of(found1, 7 + l) * local
     dev, gain = all_statistics(1, to_dev, to_gain)
     dev_out[...] = dev
     gain_out[...] = gain
-    all_means(1, to_dev)
+    packed_out[...] = mean_rows(1)
     remote.drain()
 
 
@@ -399,16 +408,19 @@
         functools.partial(filter_kernel, chunks, n_slab, n_lev, width),
         out_shape=(
             pltpu.VMEM((lev_rows, members, cols), F32),
-            pltpu.VMEM((n_lev, held, cols), BF16),
+            pltpu.VMEM((lev_rows, members, cols), BF16),
+            pltpu.VMEM((lev_rows, n_obs, cols), F32),
             pltpu.VMEM((n_obs, members), BF16),
             pltpu.VMEM((members, n_obs), BF16),
-            pltpu.VMEM((n_obs, 128), F32),
-            pltpu.VMEM((2, n_obs), F32),
+            pltpu.VMEM((n_obs, n_lev * chunks * 128), BF16),
+            pltpu.VMEM((16, n_lev * chunks * 128), BF16),
+            pltpu.VMEM((1, n_obs), F32),
             pltpu.SMEM((1,), jnp.int32),
         ),
         in_specs=[hbm] * 7,
-        out_specs=(vmem,) * 6 + (pl.BlockSpec(memory_space=pltpu.SMEM),),
+        out_specs=(vmem,) * 8 + (pl.BlockSpec(memory_space=pltpu.SMEM),),
         scratch_shapes=[
+            pltpu.VMEM((n_lev, held, cols), BF16),
             pltpu.VMEM((n_lev, held, cols), BF16),
             pltpu.VMEM(obs_cell.shape, jnp.int32),
             pltpu.VMEM(obs_cell.shape, F32),
@@ -435,51 +447,55 @@
         obs_cell, obs_value, obs_var, obs_frac, loc_level, ensemble, loc_column)))
 
 
-def last_kernel(ens, loc, dev_ref, gain_ref, level_ref, mean_ref, out_hbm, mean_hbm, out, out_sem, mean_sem):
-    lev_rows, members, cols = ens.shape
-    n_obs = dev_ref.shape[0]
+def last_kernel(
+    ens, centred, weight, dev_ref, gain_ref, place_ref, packed_ref, mean_ref,
+    out_hbm, mean_hbm, out, mean, out_sem, mean_sem,
+):
+    lev_rows = ens.shape[0]
     dev = dev_ref[...]
     gain = gain_ref[...]
-    copies = [pltpu.make_async_copy(mean_ref, mean_hbm, mean_sem)]
-    copies[0].start()
+    copies = []
     for l in range(lev_rows):
-        now = ens[l]
-        mean = jnp.sum(now, axis=0, keepdims=True) / float(members)
-        centred = (now - mean).astype(BF16)
-        cross = jnp.dot(dev, centred, preferred_element_type=F32)
-        place = LEVEL_AT + l
-        weight = level_ref[:, place : place + 1] * loc[...].reshape(n_obs, cols).astype(F32)
-        mixed = (weight * cross).astype(BF16)
-        out[l] = now + jnp.dot(gain, mixed, preferred_element_type=F32)
+        cross = jnp.dot(dev, centred[l], preferred_element_type=F32)
+        mixed = (weight[l] * cross).astype(BF16)
+        out[l] = ens[l] + jnp.dot(gain, mixed, preferred_element_type=F32)
         copies.append(pltpu.make_async_copy(out.at[l], out_hbm.at[:, l, :], out_sem.at[l]))
-        copies[l + 1].start()
+        copies[l].start()
+        if l == MEAN_AFTER:
+            mean[pl.ds(0, 1), :] = mean_ref[...]
+            mean[pl.ds(1, 1), :] = mean_of(packed_ref[...], place_ref[...])
+            mean_copy = pltpu.make_async_copy(mean, mean_hbm, mean_sem)
+            mean_copy.start()
     for copy in copies:
         copy.wait()
-
-
-LEVEL_AT = 7
+    mean_copy.wait()
+
+
+MEAN_AFTER = 3
 PIECES = 3
 VMEM_LIMIT = 40 * 1024 * 1024
 WIDTH = 2304
 COND = True
 
 
-def last_update(ens, loc, dev, gain, level, mean):
+def last_update(ens, *rest):
     lev_rows, members, cols = ens.shape
+    means = (2, rest[-1].shape[1])
     vmem = pl.BlockSpec(memory_space=pltpu.VMEM)
     hbm = pl.BlockSpec(memory_space=pltpu.HBM)
     return pl.pallas_call(
         last_kernel,
-        out_shape=(pltpu.HBM((members, lev_rows, cols), F32), pltpu.HBM(mean.shape, F32)),
-        in_specs=[vmem] * 6,
+        out_shape=(pltpu.HBM((members, lev_rows, cols), F32), pltpu.HBM(means, F32)),
+        in_specs=[vmem] * 8,
         out_specs=(hbm, hbm),
         scratch_shapes=[
             pltpu.VMEM((lev_rows, members, cols), F32),
+            pltpu.VMEM(means, F32),
             pltpu.SemaphoreType.DMA((lev_rows,)),
             pltpu.SemaphoreType.DMA,
         ],
         compiler_params=pltpu.CompilerParams(vmem_limit_bytes=VMEM_LIMIT),
-    )(*(pltpu.with_memory_space_constraint(x, pltpu.VMEM) for x in (ens, loc, dev, gain, level, mean)))
+    )(*(pltpu.with_memory_space_constraint(x, pltpu.VMEM) for x in (ens, *rest)))
 
 
 def on_device(n_slab, n_lev, ensemble, obs_cell, obs_value, obs_var, obs_frac, loc_column, loc_level):

time: 38.4 us -> 38.1 us (level)
  no operation moved by 1% of the time
where the time goes in v6:
time: 38.1 us; the launch traced here: 37.9 us
  Pallas kernels  36.9 us (97%)
  between operations  0.83 us (2%)
    pallas_call x1, Pallas kernels, run_filter(): pl.pallas_call(functools.partial(filter_kernel, chunks, n_slab, n_lev, wi...  33.3 us
    pallas_call x1, Pallas kernels, last_update(): pl.pallas_call(last_kernel, out_shape=(pltpu.HBM((members, lev_rows, cols...  3.54 us

profile of v6, /device:TPU:1, one launch (start us, length us, event | category | flops | bytes accessed | tf_op | source)
XLA Modules:
  0.0 37.9 jit_solution(10305245597717222139)
XLA Ops:
  0.6 33.3 %shard_map.86 = (f32[4,80,2304]{2,1,0:T(8,128)S(1)}, bf16[4,80,2304]{2,1,0:T(8,128)(2,1)S(1)}, f32[4,256,2304]{2,1,0:T(8,128)S(1)}, bf16[256,80]{1,0:T(8,128)(2,...) custom-call(s32[2,256]{1,0:T(2,128)} %cell_hbm.1, ...), custom_call_target="tpu_custom_call" | custom-call | tf_op jit(solution)/shard_map/pallas_call | solution.py:407
  34.0 3.5 %shard_map.87 = (f32[80,4,2304]{2,1,0:T(4,128)}, f32[2,256]{1,0:T(2,128)}) custom-call(f32[4,80,2304]{2,1,0:T(8,128)S(1)} %get-tuple-element.75.ens, bf16[4,80,2304]{2,1,0:T(8,128)(2,1)S(1)} %get-tuple-element.76.centred, f32[4,256,2304]{2,1,0:T(8,128)S(1)} %get-tuple-element.77.weight, bf16[256,80]{1,0:T(8,128)(2,1)S(1)} %get-tuple-element.78.dev_ref, ...), custom_call_target="tpu_custom_call" | custom-call | tf_op jit(solution)/shard_map/pallas_call | solution.py:486
  37.5 0.2 while.11

commit v7 on v6

--- a/solution.py
+++ b/solution.py
@@ -179,11 +179,13 @@
             pairs.append((value, var))
         return pairs
 
-    def gather_cells(places, inners):
+    def gather_cells(places, inners, arriving=None):
         index = lax.broadcasted_iota(jnp.int32, (cols, 128 * chunks), 0).astype(F32)
         hot = jnp.where(index == places, 1.0, 0.0).astype(BF16)
         cells = jnp.zeros((members, 128 * chunks), F32)
         for l in range(lev_rows):
+            if arriving is not None:
+                arriving[l].wait()
             left = jnp.concatenate(split3(ens[l])[:PIECES], axis=0)
             found = jnp.dot(left, hot, preferred_element_type=F32)
             total = found[:members]
@@ -342,9 +344,7 @@
     found0 = locate(0)
     places, inners = slot_places(found0)
     weights0 = slot_weights(found0)
-    for copy in ens_copies:
-        copy.wait()
-    _, cells = gather_cells(places, inners)
+    _, cells = gather_cells(places, inners, ens_copies)
     pl.semaphore_wait(barrier, n_lev + n_slab - 2)
     own_copies[0].wait()
     ring_begin(0)
@@ -472,7 +472,7 @@
 
 
 MEAN_AFTER = 3
-PIECES = 3
+PIECES = 2
 VMEM_LIMIT = 40 * 1024 * 1024
 WIDTH = 2304
 COND = True

time: 38.1 us -> 37.6 us (0.987)
  Pallas kernels: 36.9 us -> 36.4 us
    pallas_call x1, Pallas kernels: 33.3 us -> 32.9 us  [run_filter(): pl.pallas_call(functools.partial(filter_kernel, chunks, n_slab, n_lev, wi...]
where the time goes in v7:
time: 37.6 us; the launch traced here: 37.5 us
  Pallas kernels  36.4 us (97%)
  between operations  0.83 us (2%)
    pallas_call x1, Pallas kernels, run_filter(): pl.pallas_call(functools.partial(filter_kernel, chunks, n_slab, n_lev, wi...  32.9 us
    pallas_call x1, Pallas kernels, last_update(): pl.pallas_call(last_kernel, out_shape=(pltpu.HBM((members, lev_rows, cols...  3.54 us

profile of v7, /device:TPU:1, one launch (start us, length us, event | category | flops | bytes accessed | tf_op | source)
XLA Modules:
  0.0 37.5 jit_solution(724488626432173673)
XLA Ops:
  0.6 32.9 %shard_map.86 = (f32[4,80,2304]{2,1,0:T(8,128)S(1)}, bf16[4,80,2304]{2,1,0:T(8,128)(2,1)S(1)}, f32[4,256,2304]{2,1,0:T(8,128)S(1)}, bf16[256,80]{1,0:T(8,128)(2,...) custom-call(s32[2,256]{1,0:T(2,128)} %cell_hbm.1, ...), custom_call_target="tpu_custom_call" | custom-call | tf_op jit(solution)/shard_map/pallas_call | solution.py:407
  33.5 3.5 %shard_map.87 = (f32[80,4,2304]{2,1,0:T(4,128)}, f32[2,256]{1,0:T(2,128)}) custom-call(f32[4,80,2304]{2,1,0:T(8,128)S(1)} %get-tuple-element.75.ens, bf16[4,80,2304]{2,1,0:T(8,128)(2,1)S(1)} %get-tuple-element.76.centred, f32[4,256,2304]{2,1,0:T(8,128)S(1)} %get-tuple-element.77.weight, bf16[256,80]{1,0:T(8,128)(2,1)S(1)} %get-tuple-element.78.dev_ref, ...), custom_call_target="tpu_custom_call" | custom-call | tf_op jit(solution)/shard_map/pallas_call | solution.py:486
  37.1 0.2 while.11

commit v8 on v7

--- a/solution.py
+++ b/solution.py
@@ -94,10 +94,6 @@
         range(1, n_slab), key=lambda k: -around(k // side, side) - around(k % side, side)
     )
     lev_order = sorted(range(1, n_lev), key=lambda k: -around(k // 2, stack))
-    for k in slab_order:
-        pl.semaphore_signal(barrier, inc=1, device_id=(slab_peer[k], lev), device_id_type=MESH)
-    for k in lev_order:
-        pl.semaphore_signal(barrier, inc=1, device_id=(slab, lev_peer[k]), device_id_type=MESH)
     small_copies = [
         pltpu.make_async_copy(source, target, small_sem.at[i])
         for i, (source, target) in enumerate([
@@ -113,6 +109,10 @@
     ]
     for copy in ens_copies:
         copy.start()
+    for k in slab_order:
+        pl.semaphore_signal(barrier, inc=1, device_id=(slab_peer[k], lev), device_id_type=MESH)
+    for k in lev_order:
+        pl.semaphore_signal(barrier, inc=1, device_id=(slab, lev_peer[k]), device_id_type=MESH)
     own_copies = [
         pltpu.make_async_copy(loc_hbm.at[b], loc[b].at[lev], own_sem.at[b]) for b in range(2)
     ]
@@ -346,9 +346,9 @@
     weights0 = slot_weights(found0)
     _, cells = gather_cells(places, inners, ens_copies)
     pl.semaphore_wait(barrier, n_lev + n_slab - 2)
+    send_priors(0, cells, weights0)
     own_copies[0].wait()
     ring_begin(0)
-    send_priors(0, cells, weights0)
 
     values0 = slot_values(found0)
     found1 = locate(1)

time: 37.6 us -> 37.5 us (level)
  no operation moved by 1% of the time
where the time goes in v8:
time: 37.5 us; the launch traced here: 37.4 us
  Pallas kernels  36.4 us (97%)
  between operations  0.83 us (2%)
    pallas_call x1, Pallas kernels, run_filter(): pl.pallas_call(functools.partial(filter_kernel, chunks, n_slab, n_lev, wi...  32.8 us
    pallas_call x1, Pallas kernels, last_update(): pl.pallas_call(last_kernel, out_shape=(pltpu.HBM((members, lev_rows, cols...  3.53 us

profile of v8, /device:TPU:1, one launch (start us, length us, event | category | flops | bytes accessed | tf_op | source)
XLA Modules:
  0.0 37.4 jit_solution(8511955535793468827)
XLA Ops:
  0.6 32.8 %shard_map.86 = (f32[4,80,2304]{2,1,0:T(8,128)S(1)}, bf16[4,80,2304]{2,1,0:T(8,128)(2,1)S(1)}, f32[4,256,2304]{2,1,0:T(8,128)S(1)}, bf16[256,80]{1,0:T(8,128)(2,...) custom-call(s32[2,256]{1,0:T(2,128)} %cell_hbm.1, ...), custom_call_target="tpu_custom_call" | custom-call | tf_op jit(solution)/shard_map/pallas_call | solution.py:407
  33.5 3.5 %shard_map.87 = (f32[80,4,2304]{2,1,0:T(4,128)}, f32[2,256]{1,0:T(2,128)}) custom-call(f32[4,80,2304]{2,1,0:T(8,128)S(1)} %get-tuple-element.75.ens, bf16[4,80,2304]{2,1,0:T(8,128)(2,1)S(1)} %get-tuple-element.76.centred, f32[4,256,2304]{2,1,0:T(8,128)S(1)} %get-tuple-element.77.weight, bf16[256,80]{1,0:T(8,128)(2,1)S(1)} %get-tuple-element.78.dev_ref, ...), custom_call_target="tpu_custom_call" | custom-call | tf_op jit(solution)/shard_map/pallas_call | solution.py:486
  37.0 0.2 while.11
